TPU v7x, 32 devices: a whole 2x2x4 slice. The times are simulated.
32 devices in a mesh: clump: 8 (over z, y), grp: 4 (over x, core).
Axes of the slice: x: 2, y: 2, z: 4, core: 2. Of those that a mesh axis runs over, the one named last changes fastest.
Arguments:
- flux: float32 [32, 1024, 64], P(('clump', 'grp')), may hold values from -6 to 6
- patch_pft: int32 [32, 1024], P(('clump', 'grp')), may hold values from 0 to 15
- patch_wt: float32 [32, 1024], P(('clump', 'grp')), may hold values from 0.2 to 2
- patch_col: int32 [32, 1024], P(('clump', 'grp')), may hold values from 0 to 511, never falling along the last dimension, each value on 1 to 4 neighbouring positions
- col_wt: float32 [32, 512], P(('clump', 'grp')), may hold values from 0.2 to 2
- col_lu: int32 [32, 512], P(('clump', 'grp')), may hold values from 0 to 255, never falling along the last dimension, each value on 1 to 4 neighbouring positions
- lu_wt: float32 [32, 256], P(('clump', 'grp')), may hold values from 0.2 to 2
- lu_grid: int32 [32, 256], P(('clump', 'grp')), may hold values from 0 to 127, never falling along the last dimension, each value on 1 to 4 neighbouring positions
- cell_target: int32 [32, 128], P(('clump', 'grp')), may hold values from 0 to 4095, as said below
- patch_count: int32 [32], P(('clump', 'grp')), may hold values from 64 to 1024
- pft_scale: float32 [16, 64], replicated, may hold values from 0.3 to 3
- cpl_frac: float32 [4096], P(('clump', 'grp')), may hold values from 0.2 to 0.9
- cpl_field: float32 [4096, 64], P(('clump', 'grp')), may hold values from -6 to 6
Outputs:
- grid_merged: float32 [4096, 64], P(('clump', 'grp'))
- anomaly: float32 [32, 1024, 64], P(('clump', 'grp'))
Inputs may be any that keep to these rules, and one draw needn't show every extreme that they name: `patch_col`: within each device's row the column numbers never fall, and each column holds 1 to 4 patch slots. `col_lu`: within each device's row the landunit numbers never fall, and each landunit holds 1 to 4 columns. `lu_grid`: within each device's row the gridcell numbers never fall, and each gridcell holds 1 to 4 landunits. `cell_target`: all devices' entries together are a permutation of 0 to 4095; the coupler owner of an entry q is q // 128, and each device's 128 gridcells go to 16 owners, exactly 8 to each.
All inputs are finite; a program needn't handle non-finite values.
Results may differ from a plain program's by a relative error of at most 0.0003.
Values sent between devices are 32-bit elements; how exact they have to be, the bound alone decides.
No kernel may reach another device: no remote copies, remote signals or barrier semaphores. Data moves between devices by JAX's collectives and lax.ppermute only.
A program may use at most 64 MiB of HBM per device.

v0:
```python
import jax
import jax.numpy as jnp
from jax import lax
from jax.sharding import PartitionSpec as P

HIGH = lax.Precision.HIGHEST


def window_pick(padded, start, relative, width):
    window = lax.dynamic_slice_in_dim(padded, start, width, 0)
    onehot = (relative[:, None] == jnp.arange(width, dtype=jnp.int32)[None, :]).astype(jnp.float32)
    return jnp.dot(onehot, window, precision=HIGH)


def per_device(
    flux,
    patch_pft,
    patch_wt,
    patch_col,
    col_wt,
    col_lu,
    lu_wt,
    lu_grid,
    cell_target,
    patch_count,
    pft_scale,
    cpl_frac,
    cpl_field,
):
    n_clump = lax.axis_size("clump")
    n_group = lax.axis_size("grp")
    n_devices = n_clump * n_group
    values = flux[0]
    patches = values.shape[0]
    width_vars = values.shape[1]
    cell_count = cell_target.shape[1]
    capacity = max(2, 2 * cell_count // n_devices)
    slot_total = n_devices * capacity
    block = min(512, patches)
    blocks = patches // block
    position = jnp.arange(patches, dtype=jnp.int32)
    alive_mask = (position < patch_count[0]).astype(jnp.float32)
    type_onehot = (
        patch_pft[0][:, None] == jnp.arange(pft_scale.shape[0], dtype=jnp.int32)[None, :]
    ).astype(jnp.float32)
    scaled = values * jnp.dot(type_onehot, pft_scale, precision=HIGH)
    col_table = jnp.stack([col_wt[0], col_lu[0].astype(jnp.float32)], axis=1)
    col_table = jnp.concatenate([col_table, jnp.zeros((block, 2), jnp.float32)], axis=0)
    lu_table = jnp.stack([lu_wt[0], lu_grid[0].astype(jnp.float32)], axis=1)
    lu_table = jnp.concatenate([lu_table, jnp.zeros((block, 2), jnp.float32)], axis=0)
    within = jnp.arange(block, dtype=jnp.int32)

    def gather_block(carry, entries):
        num_acc, den_acc = carry
        cols_blk, alive_blk, pwt_blk, scaled_blk = entries
        col_start = cols_blk[0]
        col_vals = window_pick(col_table, col_start, cols_blk - col_start, block)
        land_blk = col_vals[:, 1].astype(jnp.int32)
        land_start = land_blk[0]
        lu_vals = window_pick(lu_table, land_start, land_blk - land_start, block)
        home_blk = lu_vals[:, 1].astype(jnp.int32)
        weight_blk = alive_blk * pwt_blk * col_vals[:, 0] * lu_vals[:, 0]
        home_start = home_blk[0]
        cell_onehot = (within[:, None] == (home_blk - home_start)[None, :]).astype(jnp.float32)
        part_num = jnp.dot(cell_onehot, scaled_blk * weight_blk[:, None], precision=HIGH)
        part_den = jnp.dot(cell_onehot, weight_blk, precision=HIGH)
        old_num = lax.dynamic_slice_in_dim(num_acc, home_start, block, 0)
        old_den = lax.dynamic_slice_in_dim(den_acc, home_start, block, 0)
        num_acc = lax.dynamic_update_slice_in_dim(num_acc, old_num + part_num, home_start, 0)
        den_acc = lax.dynamic_update_slice_in_dim(den_acc, old_den + part_den, home_start, 0)
        return ((num_acc, den_acc), home_blk)

    start_acc = (
        jnp.zeros((cell_count + block, width_vars), jnp.float32),
        jnp.zeros((cell_count + block,), jnp.float32),
    )
    block_inputs = (
        patch_col[0].reshape(blocks, block),
        alive_mask.reshape(blocks, block),
        patch_wt[0].reshape(blocks, block),
        scaled.reshape(blocks, block, width_vars),
    )
    (num_acc, den_acc), home_blocks = lax.scan(gather_block, start_acc, block_inputs)
    cell_num = num_acc[:cell_count]
    cell_den = den_acc[:cell_count]
    target = cell_target[0]
    owner_dev = target // cell_count
    local_slot = target - owner_dev * cell_count
    same_owner = (owner_dev[:, None] == owner_dev[None, :]).astype(jnp.int32)
    earlier = (
        jnp.arange(cell_count, dtype=jnp.int32)[None, :]
        < jnp.arange(cell_count, dtype=jnp.int32)[:, None]
    ).astype(jnp.int32)
    rank_within = jnp.sum(same_owner * earlier, axis=1)
    slot = owner_dev * capacity + rank_within
    slot_onehot = (jnp.arange(slot_total, dtype=jnp.int32)[:, None] == slot[None, :]).astype(
        jnp.float32
    )
    slot_used = jnp.sum(slot_onehot, axis=1)
    send_slot = jnp.dot(slot_onehot, local_slot.astype(jnp.float32), precision=HIGH) + (
        1.0 - slot_used
    ) * float(cell_count)
    send_slot = send_slot.reshape(n_clump, n_group, capacity)
    cell_mean = cell_num / jnp.maximum(cell_den, 1.0)[:, None]
    send_mean = jnp.dot(slot_onehot, cell_mean, precision=HIGH)
    outgoing = (send_mean.reshape(n_clump, n_group, capacity, width_vars), send_slot)
    incoming = (
        lax.all_to_all(
            lax.all_to_all(outgoing[0], "clump", split_axis=0, concat_axis=0, tiled=True),
            "grp",
            split_axis=1,
            concat_axis=1,
            tiled=True,
        ),
        lax.all_to_all(
            lax.all_to_all(outgoing[1], "clump", split_axis=0, concat_axis=0, tiled=True),
            "grp",
            split_axis=1,
            concat_axis=1,
            tiled=True,
        ),
    )
    slot_ids = incoming[-1].reshape(-1).astype(jnp.int32)
    owner_onehot = (slot_ids[:, None] == jnp.arange(cell_count, dtype=jnp.int32)[None, :]).astype(
        jnp.float32
    )
    owned_mean = jnp.dot(owner_onehot.T, incoming[0].reshape(-1, width_vars), precision=HIGH)
    grid_merged = cpl_frac[:, None] * owned_mean + (1.0 - cpl_frac)[:, None] * cpl_field
    reply_rows = jnp.dot(owner_onehot, grid_merged, precision=HIGH).reshape(
        n_clump, n_group, capacity, width_vars
    )
    returned = lax.all_to_all(
        lax.all_to_all(reply_rows, "clump", split_axis=0, concat_axis=0, tiled=True),
        "grp",
        split_axis=1,
        concat_axis=1,
        tiled=True,
    )
    cell_merged = jnp.dot(slot_onehot.T, returned.reshape(slot_total, width_vars), precision=HIGH)
    merged_table = jnp.concatenate(
        [cell_merged, jnp.zeros((block, width_vars), jnp.float32)], axis=0
    )

    def spread_block(entries):
        home_blk, alive_blk, scaled_blk = entries
        home_start = home_blk[0]
        picked = window_pick(merged_table, home_start, home_blk - home_start, block)
        return alive_blk[:, None] * (scaled_blk - picked)

    anomaly = lax.map(
        spread_block,
        (home_blocks, alive_mask.reshape(blocks, block), scaled.reshape(blocks, block, width_vars)),
    )
    return (grid_merged, anomaly.reshape(1, patches, width_vars))


def solution(mesh):
    return jax.shard_map(
        per_device,
        mesh=mesh,
        in_specs=(
            P(("clump", "grp"), None, None),
            P(("clump", "grp"), None),
            P(("clump", "grp"), None),
            P(("clump", "grp"), None),
            P(("clump", "grp"), None),
            P(("clump", "grp"), None),
            P(("clump", "grp"), None),
            P(("clump", "grp"), None),
            P(("clump", "grp"), None),
            P(("clump", "grp")),
            P(),
            P(("clump", "grp")),
            P(("clump", "grp"), None),
        ),
        out_specs=(P(("clump", "grp"), None), P(("clump", "grp"), None, None)),
        check_vma=False,
    )
```

profile of v0, /device:TPU:0, one launch (start us, length us, event | category | flops | bytes accessed | tf_op | source)
XLA Modules:
  0.0 106.9 jit_solution(788008277498538944)
XLA Ops:
  0.7 0.7 and_select_fusion
  1.9 0.7 reshape.154
  2.6 7.4 %all-to-all-start = ((f32[8,4,8]{2,1,0:T(4,128)}), f32[8,4,8]{2,1,0:T(4,128)S(1)}, u32[]{:S(2)}, u32[]{:S(2)}) async-start(f32[8,4,8]{2,1,0:T(4,128)} %reshape.154), calls=%async_computation | async-start | bytes 32768 | tf_op jit(solution)/shard_map/all_to_all | solution.py:116
  10.1 1.5 %convolution_multiply_fusion = f32[1024,64]{0,1:T(8,128)S(1)} fusion(f32[16,64]{1,0:T(8,128)S(1)} %copy-done, f32[1,1024,64]{1,2,0:T(8,128)} %param.17, s32[1024]{0:T(1024)S(1)} %bitcast.148), kind=kOutput, calls=%fused_computation.43 | convolution fusion | flops 12664832 | bytes 532480 | tf_op jit(solution)/shard_map/dot_general | solution.py:46
  12.5 0.7 copy-done.6
  13.2 0.5 broadcast.115
  13.9 0.6 reduce.6
  14.5 0.5 broadcast.116
  15.2 0.6 reduce.7
  15.9 0.7 copy-done.8
  16.5 0.7 copy-done.7
  17.2 0.7 copy-done.9
  17.9 26.6 %while.26 = (s32[]{:T(128)}, f32[640,64]{0,1:T(8,128)S(1)}, f32[640]{0:T(1024)S(1)}, s32[2,512]{1,0:T(2,128)S(1)}, s32[2,512]{1,0:T(2,128)S(1)}, /*index=5*/f32[...) while((s32[]{:T(128)}, f32[640,64]{0,1:T(8,128)S(1)}, ...), condition=%wide.region_3.4_spmd.clone, body=%wide.region_2.3_spmd.clone.sunk | while | flops 218176016 | bytes 1268031 | solution.py:83
  18.0 0.5 constant_dynamic-slice_fusion.13
  20.4 0.6 dynamic-slice_subtract_fusion.5
  21.1 0.6 fusion.62
  21.7 0.5 slice.78
  24.2 0.6 broadcast_subtract_fusion.5
  24.8 0.6 fusion.63
  25.5 0.5 slice.79
  27.9 0.6 broadcast_subtract_fusion.6
  28.8 0.7 convolution_add_fusion.2
  29.6 0.8 dynamic_update_slice.24
  30.4 0.6 fusion.65
  31.2 0.5 constant_dynamic-slice_fusion.13
  33.6 0.6 dynamic-slice_subtract_fusion.5
  34.3 0.6 fusion.62
  34.9 0.5 slice.78
  37.4 0.6 broadcast_subtract_fusion.5
  38.0 0.6 fusion.63
  38.7 0.5 slice.79
  41.2 0.6 broadcast_subtract_fusion.6
  42.1 0.8 convolution_add_fusion.2
  42.8 1.0 dynamic_update_slice.24
  43.8 0.6 fusion.65
  44.8 0.8 reshape.183
  45.6 6.0 %all-to-all-start.2 = ((f32[8,1,2048]{2,1,0:T(1,128)}), f32[8,1,2048]{2,1,0:T(1,128)S(1)}, u32[]{:S(2)}, u32[]{:S(2)}) async-start(f32[8,1,2048]{2,1,0:T(1,128)} %reshape.183), calls=%async_computation.2 | async-start | bytes 131072 | tf_op jit(solution)/shard_map/all_to_all | solution.py:109
  51.6 0.6 copy.47
  52.2 6.3 %all-to-all-done.2 = f32[8,1,2048]{2,1,0:T(1,128)S(1)} async-done(((f32[8,1,2048]{2,1,0:T(1,128)}), f32[8,1,2048]{2,1,0:T(1,128)S(1)}, u32[]{:S(2)}, u32[]{:S(2)}) %all-to-all-start.2) | async-done | bytes 65568 | tf_op jit(solution)/shard_map/all_to_all | solution.py:109
  58.5 3.3 %all-to-all-start.1 = ((f32[8,4,8]{2,0,1:T(8,128)}), f32[8,4,8]{2,0,1:T(8,128)S(1)}, u32[]{:S(2)}, u32[]{:S(2)}) async-start(f32[8,4,8]{2,0,1:T(8,128)} %copy.47), calls=%async_computation.1 | async-start | bytes 32768 | tf_op jit(solution)/shard_map/all_to_all | solution.py:115
  61.7 0.6 broadcast.121
  62.3 0.8 reduce.8
  63.2 0.8 reshape.185
  64.0 1.6 %all-to-all-done.1 = f32[8,4,8]{2,0,1:T(8,128)S(1)} async-done(((f32[8,4,8]{2,0,1:T(8,128)}), f32[8,4,8]{2,0,1:T(8,128)S(1)}, u32[]{:S(2)}, u32[]{:S(2)}) %all-to-all-start.1) | async-done | bytes 1056 | tf_op jit(solution)/shard_map/all_to_all | solution.py:115
  65.6 3.3 %all-to-all-start.3 = ((f32[4,1,4096]{2,1,0:T(1,128)}), f32[4,1,4096]{2,1,0:T(1,128)S(1)}, u32[]{:S(2)}, u32[]{:S(2)}) async-start(f32[4,1,4096]{2,1,0:T(1,128)} %reshape.185), calls=%async_computation.3 | async-start | bytes 131072 | tf_op jit(solution)/shard_map/all_to_all | solution.py:108
  69.0 3.9 %all-to-all-done.3 = f32[4,1,4096]{2,1,0:T(1,128)S(1)} async-done(((f32[4,1,4096]{2,1,0:T(1,128)}), f32[4,1,4096]{2,1,0:T(1,128)S(1)}, u32[]{:S(2)}, u32[]{:S(2)}) %all-to-all-start.3) | async-done | bytes 65568 | tf_op jit(solution)/shard_map/all_to_all | solution.py:108
  72.9 0.8 reduce.9
  73.9 0.7 copy-done.2
  75.7 9.3 %all_to_all.30 = f32[8,1,2048]{2,1,0:T(1,128)S(1)} all-to-all(f32[8,1,2048]{2,1,0:T(1,128)S(1)} %reshape.187), channel_id=1, replica_groups=mesh['clump'=8,'grp'=4] {'clump'}, dimensions={0} | all-to-all | bytes 131072 | tf_op jit(solution)/shard_map/all_to_all | solution.py:133
  85.0 0.8 reduce.10
  85.9 0.8 reshape.189
  86.6 3.3 %all-to-all-start.5 = ((f32[4,1,4096]{2,1,0:T(1,128)}), f32[4,1,4096]{2,1,0:T(1,128)S(1)}, u32[]{:S(2)}, u32[]{:S(2)}) async-start(f32[4,1,4096]{2,1,0:T(1,128)} %reshape.189), calls=%async_computation.5 | async-start | bytes 131072 | tf_op jit(solution)/shard_map/all_to_all | solution.py:132
  89.9 4.1 %all-to-all-done.5 = f32[4,1,4096]{2,1,0:T(1,128)S(1)} async-done(((f32[4,1,4096]{2,1,0:T(1,128)}), f32[4,1,4096]{2,1,0:T(1,128)S(1)}, u32[]{:S(2)}, u32[]{:S(2)}) %all-to-all-start.5) | async-done | bytes 65568 | tf_op jit(solution)/shard_map/all_to_all | solution.py:132
  94.0 0.8 reduce.11
  95.3 10.7 %while.25 = (s32[]{:T(128)}, f32[2,512,64]{1,0,2:T(2,128)S(1)}, f32[2,512]{1,0:T(2,128)S(1)}, f32[2,512,64]{1,0,2:T(2,128)S(1)}, s32[2,512]{1,0:T(2,128)S(1)}, /...) while((s32[]{:T(128)}, f32[2,512,64]{1,0,2:T(2,128)S(1)}, f32[2,512]{1,0:T(2,128)S(1)}, ...), condition=%wide.region_5.6_spmd, body=%wide.region_4.5_spmd.sunk | while | flops 201654784 | bytes 1192099 | solution.py:150
  95.3 0.5 constant_dynamic-slice_fusion.10
  97.7 0.7 dynamic-slice_subtract_fusion.4
  98.5 0.7 fusion.58
  99.4 1.2 %dynamic_update_slice.22 = f32[2,512,64]{1,0,2:T(2,128)S(1)} dynamic-update-slice(f32[2,512,64]{1,0,2:T(2,128)S(1)} %get-tuple-element.402, f32[1,512,64]{1,0,2:T(1,128)S(1)} %copy.81, s32[]{:T(128)} %get-tuple-element.401, s32[]{:T(128)} %constant.46.clone.1..sunk, s32[]{:T(128)} %constant.46.clone.1..sunk) | dynamic-update-slice | bytes 262148 | tf_op jit(solution)/shard_map/while/body/jit(dynamic_update_index_in_dim)/dynamic_update_slice | solution.py:150
  100.6 0.5 constant_dynamic-slice_fusion.10
  103.1 0.7 dynamic-slice_subtract_fusion.4
  103.9 0.7 fusion.58
  104.8 1.2 %dynamic_update_slice.22 = f32[2,512,64]{1,0,2:T(2,128)S(1)} dynamic-update-slice(f32[2,512,64]{1,0,2:T(2,128)S(1)} %get-tuple-element.402, f32[1,512,64]{1,0,2:T(1,128)S(1)} %copy.81, s32[]{:T(128)} %get-tuple-element.401, s32[]{:T(128)} %constant.46.clone.1..sunk, s32[]{:T(128)} %constant.46.clone.1..sunk) | dynamic-update-slice | bytes 262148 | tf_op jit(solution)/shard_map/while/body/jit(dynamic_update_index_in_dim)/dynamic_update_slice | solution.py:150
  106.0 0.9 reshape.160
  (77 shorter events, 4.7 us)
Async XLA Ops:
  0.6 9.4 %copy-start = (f32[16,64]{1,0:T(8,128)S(1)}, f32[16,64]{1,0:T(8,128)}, u32[]{:S(2)}) copy-start(f32[16,64]{1,0:T(8,128)} %param.27) | copy-start | bytes 12292
  0.6 0.7 copy-start.11
  2.6 7.5 %copy-start.3 = (s32[1,1024]{1,0:T(1,128)S(1)}, s32[1,1024]{1,0:T(1,128)}, u32[]{:S(2)}) copy-start(s32[1,1024]{1,0:T(1,128)} %param.18) | copy-start | bytes 12292
  2.6 42.9 %all-to-all-start = ((f32[8,4,8]{2,1,0:T(4,128)}), f32[8,4,8]{2,1,0:T(4,128)S(1)}, u32[]{:S(2)}, u32[]{:S(2)}) async-start(f32[8,4,8]{2,1,0:T(4,128)} %reshape.154), calls=%async_computation | async-start | bytes 32768 | tf_op jit(solution)/shard_map/all_to_all | solution.py:116
  12.5 0.7 copy-start.6
  13.2 0.7 copy-start.4
  14.5 0.7 copy-start.5
  15.9 0.7 copy-start.8
  16.5 0.7 copy-start.7
  17.2 0.7 copy-start.9
  45.6 12.9 %all-to-all-start.2 = ((f32[8,1,2048]{2,1,0:T(1,128)}), f32[8,1,2048]{2,1,0:T(1,128)S(1)}, u32[]{:S(2)}, u32[]{:S(2)}) async-start(f32[8,1,2048]{2,1,0:T(1,128)} %reshape.183), calls=%async_computation.2 | async-start | bytes 131072 | tf_op jit(solution)/shard_map/all_to_all | solution.py:109
  58.5 7.1 %all-to-all-start.1 = ((f32[8,4,8]{2,0,1:T(8,128)}), f32[8,4,8]{2,0,1:T(8,128)S(1)}, u32[]{:S(2)}, u32[]{:S(2)}) async-start(f32[8,4,8]{2,0,1:T(8,128)} %copy.47), calls=%async_computation.1 | async-start | bytes 32768 | tf_op jit(solution)/shard_map/all_to_all | solution.py:115
  64.0 4.9 %copy-start.10 = (f32[128]{0:T(128)S(1)}, f32[128]{0:T(128)}, u32[]{:S(2)}) copy-start(f32[128]{0:T(128)} %param.28) | copy-start | bytes 1540
  65.6 7.4 %all-to-all-start.3 = ((f32[4,1,4096]{2,1,0:T(1,128)}), f32[4,1,4096]{2,1,0:T(1,128)S(1)}, u32[]{:S(2)}, u32[]{:S(2)}) async-start(f32[4,1,4096]{2,1,0:T(1,128)} %reshape.185), calls=%async_computation.3 | async-start | bytes 131072 | tf_op jit(solution)/shard_map/all_to_all | solution.py:108
  73.9 0.8 copy-start.2
  75.0 0.6 copy-start.1
  86.6 7.4 %all-to-all-start.5 = ((f32[4,1,4096]{2,1,0:T(1,128)}), f32[4,1,4096]{2,1,0:T(1,128)S(1)}, u32[]{:S(2)}, u32[]{:S(2)}) async-start(f32[4,1,4096]{2,1,0:T(1,128)} %reshape.189), calls=%async_computation.5 | async-start | bytes 131072 | tf_op jit(solution)/shard_map/all_to_all | solution.py:132
where the time goes:
time: 108 us; the launch traced here: 107 us
  starting transfers between devices  23.3 us (22%)
  local copies, waits for them, and re-layouts  20.7 us (19%)
  waiting for transfers between devices  15.9 us (15%)
  loops' own time  15.6 us (14%)
  other arithmetic  11.2 us (10%)
  blocking collectives  9.29 us (9%)
  matrix products  9.28 us (9%)
  between operations  1.59 us (1%)
    another operation x1, loops' own time, per_device(): lax.scan(gather_block, start_acc, block_inputs)  11.6 us
    all_to_all x1, blocking collectives, per_device(): lax.all_to_all(reply_rows, 'clump', split_axis=0, concat_axis=0, tiled=True)  9.29 us
    unnamed x34, local copies, waits for them, and re-layouts  7.96 us
    all_to_all x1, starting transfers between devices, per_device(): lax.all_to_all(outgoing[1], 'clump', split_axis=0, concat_axis=0, tiled=T...  7.44 us
    all_to_all x1, waiting for transfers between devices, per_device(): lax.all_to_all(outgoing[0], 'clump', split_axis=0, concat_axis=0, tiled=T...  6.3 us
    all_to_all x1, starting transfers between devices, per_device(): lax.all_to_all(outgoing[0], 'clump', split_axis=0, concat_axis=0, tiled=T...  5.99 us
    all_to_all x1, waiting for transfers between devices, per_device(): lax.all_to_all(lax.all_to_all(reply_rows, 'clump', split_axis=0, concat_a...  4.08 us
    another operation x1, loops' own time, per_device(): lax.map(spread_block, (home_blocks, alive_mask.reshape(blocks, block), sc...  3.99 us
  transfers between devices with their start and end apart: 5, of which 4 were waited for; matrix products, arithmetic and copies ran while one was open for 22% of the time, Pallas kernels for 0%

commit v1 on v0

v1 whole, which is shorter than its diff:
```python
import functools

import jax
import jax.numpy as jnp
from jax import lax
from jax.experimental import pallas as pl
from jax.experimental.pallas import tpu as pltpu
from jax.sharding import PartitionSpec as P

AXES = ("clump", "grp")
LANES = 128
F32, BF16, I32 = jnp.float32, jnp.bfloat16, jnp.int32


def iota(shape, dim):
    return lax.broadcasted_iota(I32, shape, dim)


def split(x):
    high = x.astype(BF16)
    return high, (x - high.astype(F32)).astype(BF16)


def onehot(mask):
    return jnp.where(mask, 1.0, 0.0).astype(BF16)


def dot_nn(a, b):
    return lax.dot_general(a, b, (((1,), (0,)), ((), ())), preferred_element_type=F32)


def dot_nt(a, b):
    return lax.dot_general(a, b, (((1,), (1,)), ((), ())), preferred_element_type=F32)


def lookup(table, index):
    shape = index.shape
    lane, row = index & (LANES - 1), index >> 7
    out = None
    for r in range(table.shape[0]):
        line = jnp.broadcast_to(table[r : r + 1, :], shape)
        got = jnp.take_along_axis(line, lane, axis=1, mode="promise_in_bounds")
        out = got if out is None else jnp.where(row == r, got, out)
    return out


def as_row(x):
    return jnp.concatenate([x[s : s + 1, :] for s in range(x.shape[0])], axis=1)


def ranks(mask):
    before = onehot(iota((LANES, LANES), 0) < iota((LANES, LANES), 1))
    return dot_nn(onehot(mask), before)


def local_kernel(
    n_dev, count, flux, pft, pwt, pcol, cwt, clu, lwt, lgrid, target, scale, kept, mean, home_out, slot_out
):
    nv, patches = flux.shape
    cells = target.shape[1]
    index = pcol[...]
    land = lookup(clu[...], index)
    home = lookup(lgrid[...], land)
    weight = pwt[...] * lookup(cwt[...], index) * lookup(lwt[...], land)
    position = iota(index.shape, 0) * LANES + iota(index.shape, 1)
    alive = position < count[0]
    home = jnp.where(alive, home, -1)
    weight = jnp.where(alive, weight, 0.0)
    home_out[...] = home
    types = scale.shape[0]
    type_hot = onehot(iota((types, patches), 0) == as_row(pft[...]))
    scale_t = jnp.concatenate(split(scale[...]), axis=1).T
    factor = dot_nn(scale_t, type_hot)
    home_row = as_row(home)
    scaled = jnp.where(home_row >= 0, flux[...] * (factor[:nv] + factor[nv:]), 0.0)
    kept[...] = scaled
    weight_row = as_row(weight)
    high, low = split(scaled * weight_row)
    w_high, w_low = split(jnp.broadcast_to(weight_row, (16, patches)))
    w_both = jnp.where(iota((16, patches), 0) == 0, w_high, w_low)
    home_hot = onehot(iota((cells, patches), 0) == home_row)
    sums = dot_nt(jnp.concatenate([high, low, w_both], axis=0), home_hot)
    den = sums[2 * nv : 2 * nv + 1] + sums[2 * nv + 1 : 2 * nv + 2]
    mean[...] = (sums[:nv] + sums[nv : 2 * nv]) / jnp.maximum(den, 1.0)
    owner = target[...] // cells
    owned = iota((n_dev, cells), 0) == owner
    rank = jnp.sum(jnp.where(owned, ranks(owned), 0.0), axis=0, keepdims=True)
    slot_out[...] = rank.astype(I32) * n_dev + owner


def pack_kernel(n_dev, cap, me, heard, mean, slot, target, field, send, field_hot_out, frac_out):
    nv, cells = field.shape
    slots = n_dev * cap
    table = heard[pl.ds(0, n_dev, stride=2), :].astype(I32)
    owner = table // cells
    local = (table - owner * cells).astype(F32)
    mine = owner == me[0]
    rank = ranks(mine)
    asked = jnp.concatenate(
        [jnp.where(mine & (rank == r), local + 1.0, 0.0) for r in range(cap)], axis=0
    ).astype(BF16)
    wanted = dot_nn(asked, jnp.ones((cells, cells), BF16))
    lane = iota((slots, cells), 1)
    field_hot = onehot(wanted == (lane + 1).astype(F32))
    mean_hot = onehot(iota((slots, cells), 0) == slot[...])
    field_hot_out[...] = field_hot
    m_high, m_low = split(mean[...])
    f_high, f_low = split(field[...])
    zero = jnp.zeros((nv, 2 * cells), BF16)
    rows = jnp.concatenate(
        [
            jnp.concatenate([m_high, m_low, zero], axis=1),
            jnp.concatenate([zero, f_high, f_low], axis=1),
        ],
        axis=0,
    )
    out = dot_nt(jnp.concatenate([mean_hot, mean_hot, field_hot, field_hot], axis=1), rows)
    for r in range(cap):
        send[pl.ds(r, n_dev, stride=cap), :] = out[r * n_dev : (r + 1) * n_dev, :]
    goal = target[...]
    goal_owner = goal // cells
    goal_local = jnp.broadcast_to(goal - goal_owner * cells, (n_dev, cells))
    fracs = heard[pl.ds(1, n_dev, stride=2), :]
    picked = jnp.take_along_axis(fracs, goal_local, axis=1, mode="promise_in_bounds")
    picked = jnp.where(iota((n_dev, cells), 0) == goal_owner, picked, 0.0)
    frac_out[...] = jnp.sum(picked, axis=0, keepdims=True)


def finish_kernel(
    n_dev, cap, got, field_hot, slot, frac, mean, kept, home, own_frac, field, merged_out, anomaly_out
):
    nv, cells = field.shape
    patches = kept.shape[1]
    slots = n_dev * cap
    rows = jnp.concatenate([got[pl.ds(r, n_dev, stride=cap), :] for r in range(cap)], axis=0)
    high, low = split(rows.T)
    mean_hot = onehot(iota((slots, cells), 0) == slot[...])
    hots = jnp.concatenate([field_hot[...], mean_hot], axis=1)
    both = dot_nn(jnp.concatenate([high, low], axis=0), hots)
    width = 2 * nv
    both = both[:width] + both[width:]
    own = own_frac[...]
    merged_out[...] = own * both[:nv, :cells] + (1.0 - own) * field[...]
    part = frac[...]
    merged = part * mean[...] + (1.0 - part) * both[nv:, cells:]
    home_hot = onehot(iota((cells, patches), 0) == as_row(home[...]))
    picked = dot_nn(jnp.concatenate(split(merged), axis=0), home_hot)
    anomaly_out[...] = kept[...] - (picked[:nv] + picked[nv:])


def shape(dims, dtype=F32):
    return jax.ShapeDtypeStruct(dims, dtype)


def call(body, outs, n_args, scalars, flops):
    vmem = pl.BlockSpec(memory_space=pltpu.VMEM)
    smem = pl.BlockSpec(memory_space=pltpu.SMEM)
    return pl.pallas_call(
        body,
        out_shape=outs,
        in_specs=[smem] * scalars + [vmem] * (n_args - scalars),
        out_specs=[vmem] * len(outs),
        cost_estimate=pl.CostEstimate(flops=flops, bytes_accessed=1 << 20, transcendentals=0),
    )


def per_device(
    flux,
    patch_pft,
    patch_wt,
    patch_col,
    col_wt,
    col_lu,
    lu_wt,
    lu_grid,
    cell_target,
    patch_count,
    pft_scale,
    cpl_frac,
    cpl_field,
):
    n_dev = lax.axis_size("clump") * lax.axis_size("grp")
    patches, nv = flux.shape[1:]
    cells = cell_target.shape[1]
    cap = max(2, 2 * cells // n_dev)
    slots = n_dev * cap
    lanes = lambda x: x.reshape(-1, LANES)
    exchange = lambda x: lax.all_to_all(x, AXES, split_axis=0, concat_axis=0, tiled=True)

    frac_row = cpl_frac.reshape(1, cells)
    told = jnp.concatenate([cell_target.astype(F32), frac_row], axis=0)
    told = jnp.broadcast_to(told[None], (n_dev, 2, cells)).reshape(2 * n_dev, cells)
    heard = exchange(told)

    field_t = cpl_field.T
    kept, mean, home, slot = call(
        functools.partial(local_kernel, n_dev),
        [
            shape((nv, patches)),
            shape((nv, cells)),
            shape((patches // LANES, LANES), I32),
            shape((1, cells), I32),
        ],
        11,
        1,
        1 << 28,
    )(
        patch_count,
        flux[0].T,
        lanes(patch_pft),
        lanes(patch_wt),
        lanes(patch_col),
        lanes(col_wt),
        lanes(col_lu),
        lanes(lu_wt),
        lanes(lu_grid),
        cell_target,
        pft_scale,
    )
    me = lax.axis_index(AXES).astype(I32).reshape(1)
    send, field_hot, frac = call(
        functools.partial(pack_kernel, n_dev, cap),
        [shape((slots, 2 * nv)), shape((slots, cells), BF16), shape((1, cells))],
        6,
        1,
        1 << 26,
    )(me, heard, mean, slot, cell_target, field_t)
    got = exchange(send)
    merged, anomaly = call(
        functools.partial(finish_kernel, n_dev, cap),
        [shape((nv, cells)), shape((nv, patches))],
        9,
        0,
        1 << 26,
    )(got, field_hot, slot, frac, mean, kept, home, frac_row, field_t)
    return merged.T, anomaly.T[None]


def solution(mesh):
    split_1 = P(AXES)
    split_2 = P(AXES, None)
    split_3 = P(AXES, None, None)
    return jax.shard_map(
        per_device,
        mesh=mesh,
        in_specs=(split_3,) + (split_2,) * 8 + (split_1, P(), split_1, split_2),
        out_specs=(split_2, split_3),
        check_vma=False,
    )
```

time: 108 us -> 33.8 us (0.31)
  local copies, waits for them, and re-layouts: 20.7 us -> 1.9 us
  starting transfers between devices: 23.3 us -> 7.33 us
  loops' own time: 15.6 us -> 0 us
  waiting for transfers between devices: 15.9 us -> 4.4 us
  other arithmetic: 11.2 us -> 0.67 us
  matrix products: 9.28 us -> 0 us
  Pallas kernels: 0 us -> 6.36 us
  blocking collectives: 9.29 us -> 11.5 us
    all_to_all x5 -> x1, starting transfers between devices: 23.3 us -> 7.33 us  [per_device(): lax.all_to_all(x, AXES, split_axis=0, concat_axis=0, tiled=True)]
    another operation x2 -> x0, loops' own time: 15.6 us -> none  [the longest x1 11.6 us: per_device(): lax.scan(gather_block, start_acc, block_inputs)]
    all_to_all x5 -> x1, waiting for transfers between devices: 15.9 us -> 4.4 us  [per_device(): lax.all_to_all(x, AXES, split_axis=0, concat_axis=0, tiled=True)]
    dot_general x16 -> x0, matrix products: 9.28 us -> none  [the longest x6 3.97 us: window_pick(): return jnp.dot(onehot, window, precision=HIGH)]
    unnamed x34 -> x4, local copies, waits for them, and re-layouts: 7.96 us -> 1.27 us
    pallas_call x0 -> x3, Pallas kernels: none -> 6.36 us  [the longest x1 2.24 us: per_device(): call(functools.partial(finish_kernel, n_dev, cap), [shape((nv, cells)), s...]
    sub x9 -> x0, other arithmetic: 5.16 us -> none  [the longest x2 1.31 us: spread_block(): picked = window_pick(merged_table, home_start, home_blk - home_start, block)]
    dynamic_update_slice x8 -> x0, local copies, waits for them, and re-layouts: 4.52 us -> none  [the longest x4 2.68 us: per_device(): lax.map(spread_block, (home_blocks, alive_mask.reshape(blocks, block), sc...]
  transfers between devices with their start and end apart: 5 -> 1, of which waited for: 4 -> 1; matrix products, arithmetic and copies ran while one was open for 22% -> 0% of each run, Pallas kernels for 0% -> 7%
where the time goes in v1:
time: 33.8 us; the launch traced here: 33.4 us
  blocking collectives  11.5 us (34%)
  starting transfers between devices  7.33 us (22%)
  Pallas kernels  6.36 us (19%)
  waiting for transfers between devices  4.4 us (13%)
  local copies, waits for them, and re-layouts  1.9 us (6%)
  between operations  1.3 us (4%)
  other arithmetic  0.67 us (2%)
    all_to_all x1, blocking collectives, per_device(): lax.all_to_all(x, AXES, split_axis=0, concat_axis=0, tiled=True)  11.5 us
    all_to_all x1, starting transfers between devices, per_device(): lax.all_to_all(x, AXES, split_axis=0, concat_axis=0, tiled=True)  7.33 us
    all_to_all x1, waiting for transfers between devices, per_device(): lax.all_to_all(x, AXES, split_axis=0, concat_axis=0, tiled=True)  4.4 us
    pallas_call x1, Pallas kernels, per_device(): call(functools.partial(finish_kernel, n_dev, cap), [shape((nv, cells)), s...  2.24 us
    pallas_call x1, Pallas kernels, per_device(): call(functools.partial(local_kernel, n_dev), [shape((nv, patches)), shape...  2.2 us
    pallas_call x1, Pallas kernels, per_device(): call(functools.partial(pack_kernel, n_dev, cap), [shape((slots, 2 * nv)),...  1.92 us
    unnamed x4, local copies, waits for them, and re-layouts  1.27 us
  transfers between devices with their start and end apart: 1, of which 1 were waited for; matrix products, arithmetic and copies ran while one was open for 0% of the time, Pallas kernels for 7%

profile of v1, /device:TPU:0, one launch (start us, length us, event | category | flops | bytes accessed | tf_op | source)
XLA Modules:
  0.0 33.4 jit_solution(6938879917683119840)
XLA Ops:
  0.6 0.7 %convert_element_type.3 = f32[1,128]{1,0:T(1,128)S(1)} convert(s32[1,128]{1,0:T(1,128)} %target.3) | non-fusion elementwise | flops 128 | bytes 1024 | tf_op jit(solution)/shard_map/convert_element_type | solution.py:191
  1.3 0.0 copy-start.1
  1.3 0.7 %copy-done.1 = f32[128]{0:T(128)S(1)} copy-done((f32[128]{0:T(128)S(1)}, f32[128]{0:T(128)}, u32[]{:S(2)}) %copy-start.1) | copy-done | bytes 536
  2.0 0.6 %broadcast_in_dim.4 = f32[32,2,128]{2,1,0:T(2,128)} broadcast(f32[2,128]{1,0:T(2,128)S(1)} %pad_maximum_fusion), dimensions={1,2} | broadcast | bytes 33792 | tf_op jit(solution)/shard_map/broadcast_in_dim | solution.py:192
  2.6 7.3 %all-to-all-start = ((f32[32,2,128]{2,1,0:T(2,128)}), f32[32,2,128]{2,1,0:T(2,128)S(1)}, u32[]{:S(2)}, u32[]{:S(2)}) async-start(f32[32,2,128]{2,1,0:T(2,128)} %broadcast_in_dim.4), calls=%async_computation | async-start | bytes 65536 | tf_op jit(solution)/shard_map/all_to_all | solution.py:188
  10.6 2.2 %shard_map.140 = (f32[64,1024]{1,0:T(8,128)}, f32[64,128]{1,0:T(8,128)}, s32[8,128]{1,0:T(8,128)}, s32[1,128]{1,0:T(1,128)}) custom-call(s32[1]{0:T(128)S(6)} %copy.15.count, f32[64,1024]{1,0:T(8,128)} %bitcast.27, s32[8,128]{1,0:T(8,128)} %bitcast.30, f32[8,128]{1,0:T(8,128)} %bitcast.31, s32[8,128]{1,0:T(8,128)} %bitcast.32, f32[4,128]{1,0:T(4,128)} %bitcast.33, ...), custom_call_target="tpu_custom_call" | custom-call | flops 268435456 | bytes 1048576 | tf_op jit(solution)/shard_map/pallas_call | solution.py:196
  12.8 4.4 %all-to-all-done = f32[32,2,128]{2,1,0:T(2,128)S(1)} async-done(((f32[32,2,128]{2,1,0:T(2,128)}), f32[32,2,128]{2,1,0:T(2,128)S(1)}, u32[]{:S(2)}, u32[]{:S(2)}) %all-to-all-start) | async-done | bytes 32800 | tf_op jit(solution)/shard_map/all_to_all | solution.py:188
  17.2 0.0 copy-start
  17.2 0.6 %copy-done = f32[32,2,128]{2,1,0:T(2,128)} copy-done((f32[32,2,128]{2,1,0:T(2,128)}, f32[32,2,128]{2,1,0:T(2,128)S(1)}, u32[]{:S(2)}) %copy-start) | copy-done | bytes 32792
  17.8 1.9 %shard_map.141 = (f32[256,128]{1,0:T(8,128)}, bf16[256,128]{1,0:T(8,128)(2,1)}, f32[1,128]{1,0:T(1,128)}) custom-call(s32[1]{0:T(128)} %bitcast.me, f32[64,128]{1,0:T(8,128)} %bitcast.24, f32[64,128]{1,0:T(8,128)} %get-tuple-element.11.mean, s32[1,128]{1,0:T(1,128)} %get-tuple-element.12.slot, s32[1,128]{1,0:T(1,128)} %target.3, f32[64,128]{1,0:T(8,128)} %bitcast.22), custom_call_target="tpu_custom_call" | custom-call | flops 67108864 | bytes 1048576 | tf_op jit(solution)/shard_map/pallas_call | solution.py:221
  19.7 11.5 %all_to_all.19 = f32[32,8,128]{2,1,0:T(8,128)} all-to-all(f32[32,8,128]{2,1,0:T(8,128)} %bitcast.21), channel_id=1, replica_groups=mesh['clump'=8,'grp'=4] {'clump','grp'}, dimensions={0} | all-to-all | bytes 262144 | tf_op jit(solution)/shard_map/all_to_all | solution.py:188
  31.2 2.2 %shard_map.142 = (f32[64,128]{1,0:T(8,128)}, f32[64,1024]{1,0:T(8,128)}) custom-call(f32[256,128]{1,0:T(8,128)} %bitcast.20, bf16[256,128]{1,0:T(8,128)(2,1)} %get-tuple-element.14.field_hot, s32[1,128]{1,0:T(1,128)} %get-tuple-element.12.slot, f32[1,128]{1,0:T(1,128)} %get-tuple-element.15.frac, f32[64,128]{1,0:T(8,128)} %get-tuple-element.11.mean, ...), custom_call_target="tpu_custom_call" | custom-call | flops 67108864 | bytes 1048576 | tf_op jit(solution)/shard_map/pallas_call | solution.py:229
  (1 shorter events, 0.0 us)
Async XLA Ops:
  1.3 0.7 %copy-start.1 = (f32[128]{0:T(128)S(1)}, f32[128]{0:T(128)}, u32[]{:S(2)}) copy-start(f32[128]{0:T(128)} %param.24) | copy-start | bytes 1540
  2.6 14.6 %all-to-all-start = ((f32[32,2,128]{2,1,0:T(2,128)}), f32[32,2,128]{2,1,0:T(2,128)S(1)}, u32[]{:S(2)}, u32[]{:S(2)}) async-start(f32[32,2,128]{2,1,0:T(2,128)} %broadcast_in_dim.4), calls=%async_computation | async-start | bytes 65536 | tf_op jit(solution)/shard_map/all_to_all | solution.py:188
  17.2 0.6 %copy-start = (f32[32,2,128]{2,1,0:T(2,128)}, f32[32,2,128]{2,1,0:T(2,128)S(1)}, u32[]{:S(2)}) copy-start(f32[32,2,128]{2,1,0:T(2,128)S(1)} %all-to-all-done) | copy-start | bytes 98308

commit v2 on v1

--- a/solution.py
+++ b/solution.py
@@ -160,6 +160,7 @@
         out_shape=outs,
         in_specs=[smem] * scalars + [vmem] * (n_args - scalars),
         out_specs=[vmem] * len(outs),
+        compiler_params=pltpu.CompilerParams(vmem_limit_bytes=16 << 20),
         cost_estimate=pl.CostEstimate(flops=flops, bytes_accessed=1 << 20, transcendentals=0),
     )
 
@@ -188,9 +189,9 @@
     exchange = lambda x: lax.all_to_all(x, AXES, split_axis=0, concat_axis=0, tiled=True)
 
     frac_row = cpl_frac.reshape(1, cells)
-    told = jnp.concatenate([cell_target.astype(F32), frac_row], axis=0)
-    told = jnp.broadcast_to(told[None], (n_dev, 2, cells)).reshape(2 * n_dev, cells)
-    heard = exchange(told)
+    dims = (2 * n_dev, cells)
+    goals = jnp.broadcast_to(cell_target.astype(F32), dims)
+    heard = exchange(jnp.where(iota(dims, 0) % 2 == 0, goals, jnp.broadcast_to(frac_row, dims)))
 
     field_t = cpl_field.T
     kept, mean, home, slot = call(

time: 33.8 us -> 29.2 us (0.86)
  Pallas kernels: 6.36 us -> 2.16 us
  blocking collectives: 11.5 us -> 9.91 us
  local copies, waits for them, and re-layouts: 1.9 us -> 2.93 us
    pallas_call x1, Pallas kernels: 2.2 us -> 0.54 us  [per_device(): call(functools.partial(local_kernel, n_dev), [shape((nv, patches)), shape...]
    unnamed x4 -> x24, local copies, waits for them, and re-layouts: 1.27 us -> 2.93 us
    all_to_all x1, blocking collectives: 11.5 us -> 9.91 us  [per_device(): lax.all_to_all(x, AXES, split_axis=0, concat_axis=0, tiled=True)]
    pallas_call x1, Pallas kernels: 1.92 us -> 0.44 us  [per_device(): call(functools.partial(pack_kernel, n_dev, cap), [shape((slots, 2 * nv)),...]
    pallas_call x1, Pallas kernels: 2.24 us -> 1.19 us  [per_device(): call(functools.partial(finish_kernel, n_dev, cap), [shape((nv, cells)), s...]
    select_n x0 -> x1, other arithmetic: none -> 0.78 us  [per_device(): jnp.where(iota(dims, 0) % 2 == 0, goals, jnp.broadcast_to(frac_row, dims))]
    convert_element_type x1 -> x0, other arithmetic: 0.66 us -> none  [per_device(): told = jnp.concatenate([cell_target.astype(F32), frac_row], axis=0)]
    broadcast_in_dim x1 -> x0, local copies, waits for them, and re-layouts: 0.63 us -> none  [per_device(): jnp.broadcast_to(told[None], (n_dev, 2, cells)).reshape(2 * n_dev, cells)]
  transfers between devices with their start and end apart: 1 -> 1, of which waited for: 1 -> 1; matrix products, arithmetic and copies ran while one was open for 0% -> 0% of each run, Pallas kernels for 7% -> 2%
where the time goes in v2:
time: 29.2 us; the launch traced here: 28.9 us
  blocking collectives  9.91 us (34%)
  starting transfers between devices  7.33 us (25%)
  waiting for transfers between devices  4.29 us (15%)
  local copies, waits for them, and re-layouts  2.93 us (10%)
  Pallas kernels  2.16 us (7%)
  between operations  1.46 us (5%)
  other arithmetic  0.81 us (3%)
    all_to_all x1, blocking collectives, per_device(): lax.all_to_all(x, AXES, split_axis=0, concat_axis=0, tiled=True)  9.91 us
    all_to_all x1, starting transfers between devices, per_device(): lax.all_to_all(x, AXES, split_axis=0, concat_axis=0, tiled=True)  7.33 us
    all_to_all x1, waiting for transfers between devices, per_device(): lax.all_to_all(x, AXES, split_axis=0, concat_axis=0, tiled=True)  4.29 us
    unnamed x24, local copies, waits for them, and re-layouts  2.93 us
    pallas_call x1, Pallas kernels, per_device(): call(functools.partial(finish_kernel, n_dev, cap), [shape((nv, cells)), s...  1.19 us
    select_n x1, other arithmetic, per_device(): jnp.where(iota(dims, 0) % 2 == 0, goals, jnp.broadcast_to(frac_row, dims))  0.78 us
  transfers between devices with their start and end apart: 1, of which 1 were waited for; matrix products, arithmetic and copies ran while one was open for 0% of the time, Pallas kernels for 2%

profile of v2, /device:TPU:0, one launch (start us, length us, event | category | flops | bytes accessed | tf_op | source)
XLA Modules:
  0.0 28.9 jit_solution(6900339005734324184)
XLA Ops:
  0.6 0.0 copy-start.11
  0.7 0.6 %copy-done.11 = s32[1,128]{1,0:T(1,128)S(1)} copy-done((s32[1,128]{1,0:T(1,128)S(1)}, s32[1,128]{1,0:T(1,128)}, u32[]{:S(2)}) %copy-start.11) | copy-done | bytes 536
  1.3 0.0 copy-start.1
  1.3 0.7 %copy-done.1 = f32[128]{0:T(128)S(1)} copy-done((f32[128]{0:T(128)S(1)}, f32[128]{0:T(128)}, u32[]{:S(2)}) %copy-start.1) | copy-done | bytes 536
  2.0 0.8 %compare_select_fusion = f32[32,2,128]{2,1,0:T(2,128)} fusion(pred[32,2]{1,0:T(8,128)(4,1)S(1)} %compare_and_fusion, f32[128]{0:T(128)S(1)} %copy-done.1, f32[128]{0:T(128)S(1)} %convert_bitcast_fusion, s32[32,2]{1,0:T(8,128)S(1)} %get-tuple-element.20, s32[32,2]{1,0:T(8,128)S(1)} %get-tuple-element.21), kind=kLoop, calls=%fused_computation | loop fusion | flops 24576 | bytes 34368 | tf_op jit(solution)/shard_map/jit(_where)/select_n | solution.py:194
  2.8 7.3 %all-to-all-start = ((f32[32,2,128]{2,1,0:T(2,128)}), f32[32,2,128]{2,1,0:T(2,128)S(1)}, u32[]{:S(2)}, u32[]{:S(2)}) async-start(f32[32,2,128]{2,1,0:T(2,128)} %compare_select_fusion), calls=%async_computation | async-start | bytes 65536 | tf_op jit(solution)/shard_map/all_to_all | solution.py:189
  10.1 0.0 copy-start.8
  10.1 0.0 copy-start.9
  10.1 0.0 copy-start.10
  10.1 0.0 copy-start.7
  10.1 0.0 copy-start.6
  10.8 0.0 copy-start.5
  10.8 0.0 copy-start.3
  10.8 0.0 copy-start.4
  10.9 0.0 copy-done.8
  10.9 0.0 copy-done.9
  10.9 0.0 copy-done.10
  10.9 0.0 copy-done.7
  10.9 0.0 copy-done.6
  10.9 0.6 %copy-done.5 = f32[1,1024]{1,0:T(1,128)S(1)} copy-done((f32[1,1024]{1,0:T(1,128)S(1)}, f32[1,1024]{1,0:T(1,128)}, u32[]{:S(2)}) %copy-start.5) | copy-done | bytes 4120
  11.5 0.0 copy-done.3
  11.5 0.0 copy-done.4
  11.6 0.0 copy-start.2
  11.6 0.9 %copy-done.2 = f32[1,1024,64]{1,2,0:T(8,128)S(1)} copy-done((f32[1,1024,64]{1,2,0:T(8,128)S(1)}, f32[1,1024,64]{1,2,0:T(8,128)}, u32[]{:S(2)}) %copy-start.2) | copy-done | bytes 262168
  12.5 0.0 copy-start
  12.5 0.5 %shard_map.140 = (f32[64,1024]{1,0:T(8,128)S(1)}, f32[64,128]{1,0:T(8,128)S(1)}, s32[8,128]{1,0:T(8,128)S(1)}, s32[1,128]{1,0:T(1,128)S(1)}) custom-call(s32[1]{0:T(128)S(6)} %copy.15.count, f32[64,1024]{1,0:T(8,128)S(1)} %bitcast.28, s32[8,128]{1,0:T(8,128)S(1)} %bitcast.29, f32[8,128]{1,0:T(8,128)S(1)} %bitcast.30, s32[8,128]{1,0:T(8,128)S(1)} %bitcast.31, ...), custom_call_target="tpu_custom_call" | custom-call | flops 268435456 | bytes 1048576 | tf_op jit(solution)/shard_map/pallas_call | solution.py:197
  13.1 4.3 %all-to-all-done = f32[32,2,128]{2,1,0:T(2,128)S(1)} async-done(((f32[32,2,128]{2,1,0:T(2,128)}), f32[32,2,128]{2,1,0:T(2,128)S(1)}, u32[]{:S(2)}, u32[]{:S(2)}) %all-to-all-start) | async-done | bytes 32800 | tf_op jit(solution)/shard_map/all_to_all | solution.py:189
  17.3 0.0 copy-done
  17.3 0.4 %shard_map.141 = (f32[256,128]{1,0:T(8,128)S(1)}, bf16[256,128]{1,0:T(8,128)(2,1)S(1)}, f32[1,128]{1,0:T(1,128)S(1)}) custom-call(s32[1]{0:T(128)} %bitcast.me, f32[64,128]{1,0:T(8,128)S(1)} %bitcast.26, f32[64,128]{1,0:T(8,128)S(1)} %get-tuple-element.11.mean, s32[1,128]{1,0:T(1,128)S(1)} %get-tuple-element.12.slot, s32[1,128]{1,0:T(1,128)S(1)} %copy-done.11, ...), custom_call_target="tpu_custom_call" | custom-call | flops 67108864 | bytes 1048576 | tf_op jit(solution)/shard_map/pallas_call | solution.py:222
  17.8 9.9 %all_to_all.19 = f32[32,8,128]{2,1,0:T(8,128)S(1)} all-to-all(f32[32,8,128]{2,1,0:T(8,128)S(1)} %bitcast.23), channel_id=1, replica_groups=mesh['clump'=8,'grp'=4] {'clump','grp'}, dimensions={0} | all-to-all | bytes 262144 | tf_op jit(solution)/shard_map/all_to_all | solution.py:189
  27.7 1.2 %shard_map.142 = (f32[64,128]{1,0:T(8,128)}, f32[64,1024]{1,0:T(8,128)}) custom-call(f32[256,128]{1,0:T(8,128)S(1)} %bitcast.22, bf16[256,128]{1,0:T(8,128)(2,1)S(1)} %get-tuple-element.14.field_hot, s32[1,128]{1,0:T(1,128)S(1)} %get-tuple-element.12.slot, f32[1,128]{1,0:T(1,128)S(1)} %get-tuple-element.15.frac, f32[64,128]{1,0:T(8,128)S(1)} %get-tuple-element.11.mean, ...), custom_call_target="tpu_custom_call" | custom-call | flops 67108864 | bytes 1048576 | tf_op jit(solution)/shard_map/pallas_call | solution.py:230
  (3 shorter events, 0.0 us)
Async XLA Ops:
  0.6 0.7 %copy-start.11 = (s32[1,128]{1,0:T(1,128)S(1)}, s32[1,128]{1,0:T(1,128)}, u32[]{:S(2)}) copy-start(s32[1,128]{1,0:T(1,128)} %target.3) | copy-start | bytes 1540
  1.3 0.7 %copy-start.1 = (f32[128]{0:T(128)S(1)}, f32[128]{0:T(128)}, u32[]{:S(2)}) copy-start(f32[128]{0:T(128)} %param.24) | copy-start | bytes 1540
  2.8 14.6 %all-to-all-start = ((f32[32,2,128]{2,1,0:T(2,128)}), f32[32,2,128]{2,1,0:T(2,128)S(1)}, u32[]{:S(2)}, u32[]{:S(2)}) async-start(f32[32,2,128]{2,1,0:T(2,128)} %compare_select_fusion), calls=%async_computation | async-start | bytes 65536 | tf_op jit(solution)/shard_map/all_to_all | solution.py:189
  10.1 0.8 %copy-start.8 = (s32[1,512]{1,0:T(1,128)S(1)}, s32[1,512]{1,0:T(1,128)}, u32[]{:S(2)}) copy-start(s32[1,512]{1,0:T(1,128)} %param.18) | copy-start | bytes 6148
  10.1 0.8 %copy-start.9 = (f32[1,256]{1,0:T(1,128)S(1)}, f32[1,256]{1,0:T(1,128)}, u32[]{:S(2)}) copy-start(f32[1,256]{1,0:T(1,128)} %param.19) | copy-start | bytes 3076
  10.1 0.8 %copy-start.10 = (s32[1,256]{1,0:T(1,128)S(1)}, s32[1,256]{1,0:T(1,128)}, u32[]{:S(2)}) copy-start(s32[1,256]{1,0:T(1,128)} %param.20) | copy-start | bytes 3076
  10.1 0.8 %copy-start.7 = (f32[1,512]{1,0:T(1,128)S(1)}, f32[1,512]{1,0:T(1,128)}, u32[]{:S(2)}) copy-start(f32[1,512]{1,0:T(1,128)} %param.17) | copy-start | bytes 6148
  10.1 0.8 %copy-start.6 = (s32[1,1024]{1,0:T(1,128)S(1)}, s32[1,1024]{1,0:T(1,128)}, u32[]{:S(2)}) copy-start(s32[1,1024]{1,0:T(1,128)} %param.16) | copy-start | bytes 12292
  10.8 0.7 %copy-start.5 = (f32[1,1024]{1,0:T(1,128)S(1)}, f32[1,1024]{1,0:T(1,128)}, u32[]{:S(2)}) copy-start(f32[1,1024]{1,0:T(1,128)} %param.15) | copy-start | bytes 12292
  10.8 0.7 %copy-start.3 = (f32[16,64]{1,0:T(8,128)S(1)}, f32[16,64]{1,0:T(8,128)}, u32[]{:S(2)}) copy-start(f32[16,64]{1,0:T(8,128)} %scale.1) | copy-start | bytes 12292
  10.8 0.7 %copy-start.4 = (s32[1,1024]{1,0:T(1,128)S(1)}, s32[1,1024]{1,0:T(1,128)}, u32[]{:S(2)}) copy-start(s32[1,1024]{1,0:T(1,128)} %param.14) | copy-start | bytes 12292
  11.6 0.9 %copy-start.2 = (f32[1,1024,64]{1,2,0:T(8,128)S(1)}, f32[1,1024,64]{1,2,0:T(8,128)}, u32[]{:S(2)}) copy-start(f32[1,1024,64]{1,2,0:T(8,128)} %param.13) | copy-start | bytes 786436
  12.5 4.8 %copy-start = (f32[128,64]{0,1:T(8,128)S(1)}, f32[128,64]{0,1:T(8,128)}, u32[]{:S(2)}) copy-start(f32[128,64]{0,1:T(8,128)} %param.25) | copy-start | bytes 98308

commit v3 on v2

v3 whole, which is shorter than its diff:
```python
import functools

import jax
import jax.numpy as jnp
from jax import lax
from jax.experimental import pallas as pl
from jax.experimental.pallas import tpu as pltpu
from jax.sharding import PartitionSpec as P

AXES = ("clump", "grp")
LANES = 128
F32, BF16, I32 = jnp.float32, jnp.bfloat16, jnp.int32


def iota(shape, dim):
    return lax.broadcasted_iota(I32, shape, dim)


def split(x):
    high = x.astype(BF16)
    return high, (x - high.astype(F32)).astype(BF16)


def onehot(mask):
    return jnp.where(mask, 1.0, 0.0).astype(BF16)


def dot_nn(a, b):
    return lax.dot_general(a, b, (((1,), (0,)), ((), ())), preferred_element_type=F32)


def dot_nt(a, b):
    return lax.dot_general(a, b, (((1,), (1,)), ((), ())), preferred_element_type=F32)


def lookup(table, index):
    shape = index.shape
    lane, row = index & (LANES - 1), index >> 7
    out = None
    for r in range(table.shape[0]):
        line = jnp.broadcast_to(table[r : r + 1, :], shape)
        got = jnp.take_along_axis(line, lane, axis=1, mode="promise_in_bounds")
        out = got if out is None else jnp.where(row == r, got, out)
    return out


def as_row(x):
    return jnp.concatenate([x[s : s + 1, :] for s in range(x.shape[0])], axis=1)


def order_kernel(before):
    before[...] = onehot(iota(before.shape, 0) < iota(before.shape, 1))


def spread(hots, values):
    high, low = split(values)
    empty = jnp.zeros_like(high)
    count = len(hots)
    rows = [
        jnp.concatenate([empty, empty] * g + [high, low] + [empty, empty] * (count - 1 - g), axis=1)
        for g in range(count)
    ]
    lines = jnp.concatenate([h for hot in hots for h in (hot, hot)], axis=1)
    return dot_nt(lines, jnp.concatenate(rows, axis=0))


def unpack(got, n_dev, lines, stride, nv):
    rows = [got[pl.ds(k, n_dev, stride=stride), :] for k in range(lines)]
    flat = jnp.concatenate(rows, axis=0).T
    groups = [flat[g * nv : (g + 1) * nv] for g in range(LANES // nv)]
    return jnp.concatenate(split(jnp.concatenate(groups, axis=1)), axis=0)


def local_kernel(n_dev, cap, *refs):
    target, pcol, clu, lgrid, pwt, cwt, lwt, pft, scale, flux, frac, count, before, send, kept, slot_out, frac_out = refs
    frac_out[...] = frac[...]
    nv, patches = flux.shape
    cells = target.shape[1]
    groups = LANES // nv
    lines = cap // groups

    goal = target[...]
    owner = goal // cells
    owned = iota((n_dev, cells), 0) == owner
    rank = jnp.sum(jnp.where(owned, dot_nn(onehot(owned), before[...]), 0.0), axis=0, keepdims=True).astype(I32)
    slot = (rank % groups * lines + rank // groups) * n_dev + owner
    local = (goal - owner * cells + 1).astype(F32)
    named = jnp.where(owned, local, 0.0).astype(BF16)
    ids = dot_nt(named, onehot(iota((LANES, cells), 0) == rank)) - 1.0
    send[pl.ds(lines, n_dev, stride=lines + 1), :] = ids

    index = pcol[...]
    land = lookup(clu[...], index)
    home = lookup(lgrid[...], land)
    weight = pwt[...] * lookup(cwt[...], index) * lookup(lwt[...], land)
    position = iota(index.shape, 0) * LANES + iota(index.shape, 1)
    alive = position < count[...]
    slot_out[...] = jnp.where(alive, lookup(slot, home), -1)
    home_row = as_row(jnp.where(alive, home, -1))
    weight_row = as_row(jnp.where(alive, weight, 0.0))
    home_hot = onehot(iota((cells, patches), 0) == home_row)
    w_high, w_low = split(jnp.broadcast_to(weight_row, (16, patches)))
    w_both = jnp.where(iota((16, patches), 0) == 0, w_high, w_low)
    types = scale.shape[0]
    type_hot = onehot(iota((types, patches), 0) == as_row(pft[...]))
    scale_t = jnp.concatenate(split(scale[...]), axis=1).T
    factor = dot_nn(scale_t, type_hot)
    factor = factor[:nv] + factor[nv:]

    scaled = jnp.where(home_row >= 0, flux[...] * factor, 0.0)
    kept[...] = scaled
    high, low = split(scaled * weight_row)
    sums = dot_nt(jnp.concatenate([high, low, w_both], axis=0), home_hot)
    den = sums[2 * nv : 2 * nv + 1] + sums[2 * nv + 1 : 2 * nv + 2]
    mean = (sums[:nv] + sums[nv : 2 * nv]) / jnp.maximum(den, 1.0)
    part = lines * n_dev
    hots = [onehot(iota((part, cells), 0) + g * part == slot) for g in range(groups)]
    out = spread(hots, mean)
    for k in range(lines):
        send[pl.ds(k, n_dev, stride=lines + 1), :] = out[k * n_dev : (k + 1) * n_dev, :]


def owner_kernel(n_dev, cap, got, frac, field, send, merged_out):
    nv, cells = field.shape
    groups = LANES // nv
    lines = cap // groups
    ids = got[pl.ds(lines, n_dev, stride=lines + 1), :]
    lane = iota((n_dev, cells), 1).astype(F32)
    hots = []
    for g in range(groups):
        named = [ids[:, k * groups + g : k * groups + g + 1] for k in range(lines)]
        hots.append(jnp.concatenate([onehot(lane == column) for column in named], axis=0))
    means = unpack(got, n_dev, lines, lines + 1, nv)
    placed = dot_nn(means, jnp.concatenate(hots, axis=0))
    part = frac[...]
    merged = part * (placed[:nv] + placed[nv:]) + (1.0 - part) * field[...]
    merged_out[...] = merged
    out = spread(hots, merged)
    for k in range(lines):
        send[pl.ds(k, n_dev, stride=lines), :] = out[k * n_dev : (k + 1) * n_dev, :]


def finish_kernel(n_dev, cap, got, slot, kept, merged, merged_out, anomaly_out):
    merged_out[...] = merged[...]
    nv, patches = kept.shape
    lines = cap * nv // LANES
    replies = unpack(got, n_dev, lines, lines, nv)
    hot = onehot(iota((n_dev * cap, patches), 0) == as_row(slot[...]))
    picked = dot_nn(replies, hot)
    anomaly_out[...] = kept[...] - (picked[:nv] + picked[nv:])


def shape(dims, dtype=F32):
    return jax.ShapeDtypeStruct(dims, dtype)


VMEM = pl.BlockSpec(memory_space=pltpu.VMEM)


def call(body, outs, in_specs, flops, scratch=()):
    return pl.pallas_call(
        body,
        out_shape=outs,
        in_specs=in_specs,
        out_specs=[VMEM] * len(outs),
        scratch_shapes=list(scratch),
        compiler_params=pltpu.CompilerParams(vmem_limit_bytes=16 << 20),
        cost_estimate=pl.CostEstimate(flops=flops, bytes_accessed=1 << 20, transcendentals=0),
    )


def per_device(
    flux,
    patch_pft,
    patch_wt,
    patch_col,
    col_wt,
    col_lu,
    lu_wt,
    lu_grid,
    cell_target,
    patch_count,
    pft_scale,
    cpl_frac,
    cpl_field,
):
    n_dev = lax.axis_size("clump") * lax.axis_size("grp")
    patches, nv = flux.shape[1:]
    cells = cell_target.shape[1]
    cap = max(2, 2 * cells // n_dev)
    lines = cap * nv // LANES
    lanes = lambda x: x.reshape(-1, LANES)

    def exchange(x):
        rows = x.shape[0] // n_dev
        x = x.reshape(n_dev, 1, rows * LANES)
        return lax.all_to_all(x, AXES, split_axis=0, concat_axis=0, tiled=True).reshape(-1, LANES)

    inputs = [
        cell_target,
        lanes(patch_col),
        lanes(col_lu),
        lanes(lu_grid),
        lanes(patch_wt),
        lanes(col_wt),
        lanes(lu_wt),
        lanes(patch_pft),
        pft_scale,
        flux[0].T,
        cpl_frac.reshape(1, cells),
        patch_count.reshape(1, 1),
    ]
    (before,) = call(order_kernel, [shape((cells, cells), BF16)], [], 1 << 33)()
    inputs.append(before)
    send, kept, slot, frac = call(
        functools.partial(local_kernel, n_dev, cap),
        [
            shape((n_dev * (lines + 1), LANES)),
            shape((nv, patches)),
            shape((patches // LANES, LANES), I32),
            shape((1, cells)),
        ],
        [VMEM] * len(inputs),
        1 << 26,
    )(*inputs)
    reply, merged = call(
        functools.partial(owner_kernel, n_dev, cap),
        [shape((n_dev * lines, LANES)), shape((nv, cells))],
        [VMEM] * 3,
        1 << 26,
    )(exchange(send), frac, cpl_field.T)
    merged, anomaly = call(
        functools.partial(finish_kernel, n_dev, cap),
        [shape((nv, cells)), shape((nv, patches))],
        [VMEM] * 4,
        1 << 26,
    )(exchange(reply), slot, kept, merged)
    return merged.T, anomaly.T[None]


def solution(mesh):
    split_1 = P(AXES)
    split_2 = P(AXES, None)
    split_3 = P(AXES, None, None)
    return jax.shard_map(
        per_device,
        mesh=mesh,
        in_specs=(split_3,) + (split_2,) * 8 + (split_1, P(), split_1, split_2),
        out_specs=(split_2, split_3),
        check_vma=False,
    )
```

time: 29.2 us -> 28.6 us (0.979)
  blocking collectives: 9.91 us -> 23.8 us
  starting transfers between devices: 7.33 us -> 0 us
  waiting for transfers between devices: 4.29 us -> 0 us
  local copies, waits for them, and re-layouts: 2.93 us -> 0.72 us
  other arithmetic: 0.81 us -> 0 us
    all_to_all x1 -> x2, blocking collectives: 9.91 us -> 23.8 us  [exchange(): lax.all_to_all(x, AXES, split_axis=0, concat_axis=0, tiled=True)]
    all_to_all x1 -> x0, starting transfers between devices: 7.33 us -> none  [per_device(): lax.all_to_all(x, AXES, split_axis=0, concat_axis=0, tiled=True)]
    all_to_all x1 -> x0, waiting for transfers between devices: 4.29 us -> none  [per_device(): lax.all_to_all(x, AXES, split_axis=0, concat_axis=0, tiled=True)]
    unnamed x24, local copies, waits for them, and re-layouts: 2.93 us -> 0.72 us
    select_n x1 -> x0, other arithmetic: 0.78 us -> none  [per_device(): jnp.where(iota(dims, 0) % 2 == 0, goals, jnp.broadcast_to(frac_row, dims))]
    pallas_call x2 -> x3, Pallas kernels: 0.98 us -> 1.28 us  [the longest x1 0.8 us: per_device(): call(functools.partial(local_kernel, n_dev, cap), [shape((n_dev * (lines...]
  transfers between devices with their start and end apart: 1 -> 0, of which waited for: 1 -> 0; matrix products, arithmetic and copies ran while one was open for 0% -> 0% of each run, Pallas kernels for 2% -> 0%
where the time goes in v3:
time: 28.6 us; the launch traced here: 28.3 us
  blocking collectives  23.8 us (83%)
  Pallas kernels  2.31 us (8%)
  between operations  1.5 us (5%)
  local copies, waits for them, and re-layouts  0.72 us (3%)
    all_to_all x2, blocking collectives, exchange(): lax.all_to_all(x, AXES, split_axis=0, concat_axis=0, tiled=True)  23.8 us
    pallas_call x1, Pallas kernels, per_device(): call(functools.partial(finish_kernel, n_dev, cap), [shape((nv, cells)), s...  1.02 us
    pallas_call x1, Pallas kernels, per_device(): call(functools.partial(local_kernel, n_dev, cap), [shape((n_dev * (lines...  0.8 us
    unnamed x24, local copies, waits for them, and re-layouts  0.72 us

profile of v3, /device:TPU:0, one launch (start us, length us, event | category | flops | bytes accessed | tf_op | source)
XLA Modules:
  0.0 28.3 jit_solution(464328551850841653)
XLA Ops:
  0.6 0.0 copy-start
  0.6 0.0 copy-start.3
  0.7 0.0 copy-start.4
  0.7 0.0 copy-start.6
  0.7 0.0 copy-start.8
  0.7 0.0 copy-start.9
  0.7 0.0 copy-start.10
  1.5 0.0 copy-start.1
  1.5 0.0 copy-start.2
  1.5 0.0 copy-start.5
  1.5 0.0 copy-start.7
  1.5 0.1 copy-done
  1.6 0.0 copy-done.3
  1.6 0.0 copy-done.4
  1.6 0.0 copy-done.6
  1.6 0.0 copy-done.8
  1.6 0.0 copy-done.9
  1.6 0.0 copy-done.10
  1.6 0.6 %copy-done.1 = f32[16,64]{1,0:T(8,128)S(1)} copy-done((f32[16,64]{1,0:T(8,128)S(1)}, f32[16,64]{1,0:T(8,128)}, u32[]{:S(2)}) %copy-start.1) | copy-done | bytes 4120
  2.2 0.0 copy-done.2
  2.2 0.0 copy-done.5
  2.2 0.0 copy-done.7
  2.2 0.8 %shard_map.141 = (f32[160,128]{1,0:T(8,128)S(1)}, f32[64,1024]{1,0:T(8,128)S(1)}, s32[8,128]{1,0:T(8,128)S(1)}, f32[1,128]{1,0:T(1,128)S(1)}) custom-call(s32[1,128]{1,0:T(1,128)S(1)} %copy-done.9, s32[8,128]{1,0:T(8,128)S(1)} %bitcast.27, s32[4,128]{1,0:T(4,128)S(1)} %bitcast.30, s32[2,128]{1,0:T(2,128)S(1)} %bitcast.32, f32[8,128]{1,0:T(8,128)S(1)} %bitcast.28, ...), custom_call_target="tpu_custom_call" | custom-call | flops 67108864 | bytes 1048576 | tf_op jit(solution)/shard_map/pallas_call | solution.py:215
  3.0 0.0 copy-start.11
  3.0 14.7 %all_to_all.10 = f32[32,1,640]{2,1,0:T(1,128)S(1)} all-to-all(f32[32,1,640]{2,1,0:T(1,128)S(1)} %bitcast.24), channel_id=1, replica_groups=mesh['clump'=8,'grp'=4] {'clump','grp'}, dimensions={0} | all-to-all | bytes 163840 | tf_op jit(solution)/shard_map/all_to_all | solution.py:197
  17.7 0.0 copy-done.11
  17.7 0.5 %shard_map.142 = (f32[128,128]{1,0:T(8,128)S(1)}, f32[64,128]{1,0:T(8,128)S(1)}) custom-call(f32[160,128]{1,0:T(8,128)S(1)} %bitcast.25, f32[1,128]{1,0:T(1,128)S(1)} %get-tuple-element.11.frac, f32[64,128]{1,0:T(8,128)S(1)} %bitcast.35), custom_call_target="tpu_custom_call" | custom-call | flops 67108864 | bytes 1048576 | tf_op jit(solution)/shard_map/pallas_call | solution.py:226
  18.2 9.1 %all_to_all.11 = f32[32,1,512]{2,1,0:T(1,128)S(1)} all-to-all(f32[32,1,512]{2,1,0:T(1,128)S(1)} %bitcast.26), channel_id=1, replica_groups=mesh['clump'=8,'grp'=4] {'clump','grp'}, dimensions={0} | all-to-all | bytes 131072 | tf_op jit(solution)/shard_map/all_to_all | solution.py:197
  27.3 1.0 %shard_map.143 = (f32[64,128]{1,0:T(8,128)}, f32[64,1024]{1,0:T(8,128)}) custom-call(f32[128,128]{1,0:T(8,128)S(1)} %bitcast.23, s32[8,128]{1,0:T(8,128)S(1)} %get-tuple-element.13.slot, f32[64,1024]{1,0:T(8,128)S(1)} %get-tuple-element.14.kept, f32[64,128]{1,0:T(8,128)S(1)} %get-tuple-element.15.merged), custom_call_target="tpu_custom_call" | custom-call | flops 67108864 | bytes 1048576 | tf_op jit(solution)/shard_map/pallas_call | solution.py:232
  (1 shorter events, 0.0 us)
Async XLA Ops:
  0.6 1.0 %copy-start = (f32[1,1024,64]{1,2,0:T(8,128)S(1)}, f32[1,1024,64]{1,2,0:T(8,128)}, u32[]{:S(2)}) copy-start(f32[1,1024,64]{1,2,0:T(8,128)} %param.13) | copy-start | bytes 786436
  0.6 0.9 %copy-start.3 = (f32[1,1024]{1,0:T(1,128)S(1)}, f32[1,1024]{1,0:T(1,128)}, u32[]{:S(2)}) copy-start(f32[1,1024]{1,0:T(1,128)} %param.15) | copy-start | bytes 12292
  0.7 0.9 %copy-start.4 = (s32[1,1024]{1,0:T(1,128)S(1)}, s32[1,1024]{1,0:T(1,128)}, u32[]{:S(2)}) copy-start(s32[1,1024]{1,0:T(1,128)} %param.14) | copy-start | bytes 12292
  0.7 0.9 %copy-start.6 = (f32[1,512]{1,0:T(1,128)S(1)}, f32[1,512]{1,0:T(1,128)}, u32[]{:S(2)}) copy-start(f32[1,512]{1,0:T(1,128)} %param.17) | copy-start | bytes 6148
  0.7 0.9 %copy-start.8 = (f32[1,256]{1,0:T(1,128)S(1)}, f32[1,256]{1,0:T(1,128)}, u32[]{:S(2)}) copy-start(f32[1,256]{1,0:T(1,128)} %param.19) | copy-start | bytes 3076
  0.7 0.9 %copy-start.9 = (s32[1,128]{1,0:T(1,128)S(1)}, s32[1,128]{1,0:T(1,128)}, u32[]{:S(2)}) copy-start(s32[1,128]{1,0:T(1,128)} %refs_0_.1) | copy-start | bytes 1540
  0.7 0.9 %copy-start.10 = (f32[128]{0:T(128)S(1)}, f32[128]{0:T(128)}, u32[]{:S(2)}) copy-start(f32[128]{0:T(128)} %param.24) | copy-start | bytes 1540
  1.5 0.7 %copy-start.1 = (f32[16,64]{1,0:T(8,128)S(1)}, f32[16,64]{1,0:T(8,128)}, u32[]{:S(2)}) copy-start(f32[16,64]{1,0:T(8,128)} %refs_8_.1) | copy-start | bytes 12292
  1.5 0.7 %copy-start.2 = (s32[1,1024]{1,0:T(1,128)S(1)}, s32[1,1024]{1,0:T(1,128)}, u32[]{:S(2)}) copy-start(s32[1,1024]{1,0:T(1,128)} %param.16) | copy-start | bytes 12292
  1.5 0.7 %copy-start.5 = (s32[1,512]{1,0:T(1,128)S(1)}, s32[1,512]{1,0:T(1,128)}, u32[]{:S(2)}) copy-start(s32[1,512]{1,0:T(1,128)} %param.18) | copy-start | bytes 6148
  1.5 0.7 %copy-start.7 = (s32[1,256]{1,0:T(1,128)S(1)}, s32[1,256]{1,0:T(1,128)}, u32[]{:S(2)}) copy-start(s32[1,256]{1,0:T(1,128)} %param.20) | copy-start | bytes 3076
  3.0 14.7 %copy-start.11 = (f32[128,64]{0,1:T(8,128)S(1)}, f32[128,64]{0,1:T(8,128)}, u32[]{:S(2)}) copy-start(f32[128,64]{0,1:T(8,128)} %param.25) | copy-start | bytes 98308

commit v4 on v3

--- a/solution.py
+++ b/solution.py
@@ -9,6 +9,7 @@
 
 AXES = ("clump", "grp")
 LANES = 128
+PIECE = 256
 F32, BF16, I32 = jnp.float32, jnp.bfloat16, jnp.int32
 
 
@@ -71,23 +72,35 @@
     return jnp.concatenate(split(jnp.concatenate(groups, axis=1)), axis=0)
 
 
-def local_kernel(n_dev, cap, *refs):
-    target, pcol, clu, lgrid, pwt, cwt, lwt, pft, scale, flux, frac, count, before, send, kept, slot_out, frac_out = refs
+def prepare_kernel(
+    n_dev,
+    cap,
+    pcol,
+    clu,
+    lgrid,
+    pwt,
+    cwt,
+    lwt,
+    count,
+    target,
+    pft,
+    scale,
+    frac,
+    before,
+    live_scale,
+    sum_scale,
+    home_hot,
+    weights,
+    slot_hot,
+    ids,
+    slot_out,
+    frac_out,
+):
     frac_out[...] = frac[...]
-    nv, patches = flux.shape
-    cells = target.shape[1]
+    cells, patches = home_hot.shape
+    nv = live_scale.shape[0]
     groups = LANES // nv
     lines = cap // groups
-
-    goal = target[...]
-    owner = goal // cells
-    owned = iota((n_dev, cells), 0) == owner
-    rank = jnp.sum(jnp.where(owned, dot_nn(onehot(owned), before[...]), 0.0), axis=0, keepdims=True).astype(I32)
-    slot = (rank % groups * lines + rank // groups) * n_dev + owner
-    local = (goal - owner * cells + 1).astype(F32)
-    named = jnp.where(owned, local, 0.0).astype(BF16)
-    ids = dot_nt(named, onehot(iota((LANES, cells), 0) == rank)) - 1.0
-    send[pl.ds(lines, n_dev, stride=lines + 1), :] = ids
 
     index = pcol[...]
     land = lookup(clu[...], index)
@@ -95,27 +108,48 @@
     weight = pwt[...] * lookup(cwt[...], index) * lookup(lwt[...], land)
     position = iota(index.shape, 0) * LANES + iota(index.shape, 1)
     alive = position < count[...]
+
+    goal = target[...]
+    owner = goal // cells
+    owned = iota((n_dev, cells), 0) == owner
+    rank = jnp.sum(jnp.where(owned, dot_nn(onehot(owned), before[...]), 0.0), axis=0, keepdims=True)
+    rank = rank.astype(I32)
+    slot = (rank % groups * lines + rank // groups) * n_dev + owner
+    local = (goal - owner * cells + 1).astype(F32)
+    named = jnp.where(owned, local, 0.0).astype(BF16)
+    ids[...] = dot_nt(named, onehot(iota((LANES, cells), 0) == rank)) - 1.0
+    slot_hot[...] = onehot(iota(slot_hot.shape, 0) == slot)
     slot_out[...] = jnp.where(alive, lookup(slot, home), -1)
-    home_row = as_row(jnp.where(alive, home, -1))
-    weight_row = as_row(jnp.where(alive, weight, 0.0))
-    home_hot = onehot(iota((cells, patches), 0) == home_row)
-    w_high, w_low = split(jnp.broadcast_to(weight_row, (16, patches)))
-    w_both = jnp.where(iota((16, patches), 0) == 0, w_high, w_low)
+
     types = scale.shape[0]
     type_hot = onehot(iota((types, patches), 0) == as_row(pft[...]))
     scale_t = jnp.concatenate(split(scale[...]), axis=1).T
     factor = dot_nn(scale_t, type_hot)
     factor = factor[:nv] + factor[nv:]
-
-    scaled = jnp.where(home_row >= 0, flux[...] * factor, 0.0)
-    kept[...] = scaled
-    high, low = split(scaled * weight_row)
-    sums = dot_nt(jnp.concatenate([high, low, w_both], axis=0), home_hot)
+    home_row = as_row(jnp.where(alive, home, -1))
+    weight_row = as_row(jnp.where(alive, weight, 0.0))
+    live_scale[...] = jnp.where(home_row >= 0, factor, 0.0)
+    sum_scale[...] = factor * weight_row
+    home_hot[...] = onehot(iota((cells, patches), 0) == home_row)
+    w_high, w_low = split(jnp.broadcast_to(weight_row, weights.shape))
+    weights[...] = jnp.where(iota(weights.shape, 0) == 0, w_high, w_low)
+
+
+def local_kernel(
+    n_dev, flux, live_scale, sum_scale, home_hot, weights, slot_hot, ids, send, kept
+):
+    nv = flux.shape[0]
+    groups = LANES // nv
+    part = slot_hot.shape[0] // groups
+    lines = part // n_dev
+    values = flux[...]
+    high, low = split(values * sum_scale[...])
+    sums = dot_nt(jnp.concatenate([high, low, weights[...]], axis=0), home_hot[...])
+    kept[...] = values * live_scale[...]
+    send[pl.ds(lines, n_dev, stride=lines + 1), :] = ids[...]
     den = sums[2 * nv : 2 * nv + 1] + sums[2 * nv + 1 : 2 * nv + 2]
     mean = (sums[:nv] + sums[nv : 2 * nv]) / jnp.maximum(den, 1.0)
-    part = lines * n_dev
-    hots = [onehot(iota((part, cells), 0) + g * part == slot) for g in range(groups)]
-    out = spread(hots, mean)
+    out = spread([slot_hot[g * part : (g + 1) * part, :] for g in range(groups)], mean)
     for k in range(lines):
         send[pl.ds(k, n_dev, stride=lines + 1), :] = out[k * n_dev : (k + 1) * n_dev, :]
 
@@ -130,24 +164,36 @@
     for g in range(groups):
         named = [ids[:, k * groups + g : k * groups + g + 1] for k in range(lines)]
         hots.append(jnp.concatenate([onehot(lane == column) for column in named], axis=0))
+    part = frac[...]
+    rest = (1.0 - part) * field[...]
+    own = spread(hots, jnp.broadcast_to(part, (nv, cells)))
+    other = spread(hots, rest)
+    for k in range(lines):
+        at = slice(k * n_dev, (k + 1) * n_dev)
+        row = got[pl.ds(k, n_dev, stride=lines + 1), :]
+        send[pl.ds(k, n_dev, stride=lines), :] = own[at, :] * row + other[at, :]
     means = unpack(got, n_dev, lines, lines + 1, nv)
     placed = dot_nn(means, jnp.concatenate(hots, axis=0))
-    part = frac[...]
-    merged = part * (placed[:nv] + placed[nv:]) + (1.0 - part) * field[...]
-    merged_out[...] = merged
-    out = spread(hots, merged)
-    for k in range(lines):
-        send[pl.ds(k, n_dev, stride=lines), :] = out[k * n_dev : (k + 1) * n_dev, :]
-
-
-def finish_kernel(n_dev, cap, got, slot, kept, merged, merged_out, anomaly_out):
-    merged_out[...] = merged[...]
+    merged_out[...] = part * (placed[:nv] + placed[nv:]) + rest
+
+
+def finish_kernel(n_dev, cap, got, slot, kept, merged, merged_out, anomaly_out, buffer, sem):
     nv, patches = kept.shape
+    pieces = buffer.shape[1] // PIECE
+    copies = [pltpu.make_async_copy(merged, merged_out, sem.at[pieces])]
+    copies[0].start()
     lines = cap * nv // LANES
     replies = unpack(got, n_dev, lines, lines, nv)
-    hot = onehot(iota((n_dev * cap, patches), 0) == as_row(slot[...]))
-    picked = dot_nn(replies, hot)
-    anomaly_out[...] = kept[...] - (picked[:nv] + picked[nv:])
+    row = as_row(slot[...])
+    for c in range(pieces):
+        at = slice(c * PIECE, (c + 1) * PIECE)
+        hot = onehot(iota((n_dev * cap, PIECE), 0) == row[:, at])
+        picked = dot_nn(replies, hot)
+        buffer[:, at] = kept[:, at] - (picked[:nv] + picked[nv:])
+        copies.append(pltpu.make_async_copy(buffer.at[:, at], anomaly_out.at[:, at], sem.at[c]))
+        copies[-1].start()
+    for copy in copies:
+        copy.wait()
 
 
 def shape(dims, dtype=F32):
@@ -155,14 +201,15 @@
 
 
 VMEM = pl.BlockSpec(memory_space=pltpu.VMEM)
-
-
-def call(body, outs, in_specs, flops, scratch=()):
+HBM = pl.BlockSpec(memory_space=pltpu.HBM)
+
+
+def call(body, outs, in_specs, flops, scratch=(), space=None):
     return pl.pallas_call(
         body,
         out_shape=outs,
         in_specs=in_specs,
-        out_specs=[VMEM] * len(outs),
+        out_specs=[space or VMEM] * len(outs),
         scratch_shapes=list(scratch),
         compiler_params=pltpu.CompilerParams(vmem_limit_bytes=16 << 20),
         cost_estimate=pl.CostEstimate(flops=flops, bytes_accessed=1 << 20, transcendentals=0),
@@ -196,33 +243,41 @@
         x = x.reshape(n_dev, 1, rows * LANES)
         return lax.all_to_all(x, AXES, split_axis=0, concat_axis=0, tiled=True).reshape(-1, LANES)
 
-    inputs = [
-        cell_target,
+    (before,) = call(order_kernel, [shape((cells, cells), BF16)], [], 1 << 29)()
+    *plan, slot, frac = call(
+        functools.partial(prepare_kernel, n_dev, cap),
+        [
+            shape((nv, patches)),
+            shape((nv, patches)),
+            shape((cells, patches), BF16),
+            shape((16, patches), BF16),
+            shape((n_dev * cap, cells), BF16),
+            shape((n_dev, LANES)),
+            shape((patches // LANES, LANES), I32),
+            shape((1, cells)),
+        ],
+        [VMEM] * 12,
+        1 << 26,
+    )(
         lanes(patch_col),
         lanes(col_lu),
         lanes(lu_grid),
         lanes(patch_wt),
         lanes(col_wt),
         lanes(lu_wt),
+        patch_count.reshape(1, 1),
+        cell_target,
         lanes(patch_pft),
         pft_scale,
-        flux[0].T,
         cpl_frac.reshape(1, cells),
-        patch_count.reshape(1, 1),
-    ]
-    (before,) = call(order_kernel, [shape((cells, cells), BF16)], [], 1 << 33)()
-    inputs.append(before)
-    send, kept, slot, frac = call(
-        functools.partial(local_kernel, n_dev, cap),
-        [
-            shape((n_dev * (lines + 1), LANES)),
-            shape((nv, patches)),
-            shape((patches // LANES, LANES), I32),
-            shape((1, cells)),
-        ],
-        [VMEM] * len(inputs),
+        before,
+    )
+    send, kept = call(
+        functools.partial(local_kernel, n_dev),
+        [shape((n_dev * (lines + 1), LANES)), shape((nv, patches))],
+        [VMEM] * 7,
         1 << 26,
-    )(*inputs)
+    )(flux[0].T, *plan)
     reply, merged = call(
         functools.partial(owner_kernel, n_dev, cap),
         [shape((n_dev * lines, LANES)), shape((nv, cells))],
@@ -234,6 +289,8 @@
         [shape((nv, cells)), shape((nv, patches))],
         [VMEM] * 4,
         1 << 26,
+        [pltpu.VMEM((nv, patches), F32), pltpu.SemaphoreType.DMA((patches // PIECE + 1,))],
+        HBM,
     )(exchange(reply), slot, kept, merged)
     return merged.T, anomaly.T[None]
 

time: 28.6 us -> 27.9 us (0.976)
  local copies, waits for them, and re-layouts: 0.72 us -> 0.05 us
    unnamed x24, local copies, waits for them, and re-layouts: 0.72 us -> 0.05 us
    pallas_call x2 -> x3, Pallas kernels: 0.81 us -> 0.91 us  [the longest x1 0.49 us: per_device(): call(functools.partial(local_kernel, n_dev), [shape((n_dev * (lines + 1),...]
where the time goes in v4:
time: 27.9 us; the launch traced here: 27.6 us
  blocking collectives  23.8 us (85%)
  Pallas kernels  2.23 us (8%)
  between operations  1.53 us (5%)
    all_to_all x2, blocking collectives, exchange(): lax.all_to_all(x, AXES, split_axis=0, concat_axis=0, tiled=True)  23.8 us
    pallas_call x1, Pallas kernels, per_device(): call(functools.partial(finish_kernel, n_dev, cap), [shape((nv, cells)), s...  1.01 us

profile of v4, /device:TPU:0, one launch (start us, length us, event | category | flops | bytes accessed | tf_op | source)
XLA Modules:
  0.0 27.6 jit_solution(10580820289783985504)
XLA Ops:
  0.6 0.0 copy-start.2
  0.6 0.0 copy-start.3
  0.7 0.0 copy-start.4
  0.7 0.0 copy-start.5
  0.7 0.0 copy-start.6
  0.7 0.0 copy-start.7
  0.7 0.0 copy-start.8
  0.7 0.0 copy-start.9
  0.7 0.0 copy-start.10
  0.7 0.0 copy-start.11
  0.8 0.0 copy-start
  1.5 0.0 copy-done.2
  1.5 0.0 copy-done.3
  1.5 0.0 copy-done.4
  1.5 0.0 copy-done.5
  1.5 0.0 copy-done.6
  1.5 0.0 copy-done.7
  1.5 0.0 copy-done.8
  1.5 0.0 copy-done.9
  1.5 0.0 copy-done.10
  1.5 0.0 copy-done.11
  1.6 0.4 %shard_map.141 = (f32[64,1024]{1,0:T(8,128)S(1)}, f32[64,1024]{1,0:T(8,128)S(1)}, bf16[128,1024]{1,0:T(8,128)(2,1)S(1)}, bf16[16,1024]{1,0:T(8,128)(2,1)S(1)}, b...) custom-call(s32[8,128]{1,0:T(8,128)S(1)} %bitcast.28, ...), custom_call_target="tpu_custom_call" | custom-call | flops 67108864 | bytes 1048576 | tf_op jit(solution)/shard_map/pallas_call | solution.py:247
  2.0 0.0 copy-done
  2.0 0.5 %shard_map.142 = (f32[160,128]{1,0:T(8,128)S(1)}, f32[64,1024]{1,0:T(8,128)S(1)}) custom-call(f32[64,1024]{1,0:T(8,128)S(1)} %bitcast.23, f32[64,1024]{1,0:T(8,128)S(1)} %get-tuple-element.16.live_scale, f32[64,1024]{1,0:T(8,128)S(1)} %get-tuple-element.17.sum_scale, bf16[128,1024]{1,0:T(8,128)(2,1)S(1)} %get-tuple-element.18.home_hot, ...), custom_call_target="tpu_custom_call" | custom-call | flops 67108864 | bytes 1048576 | tf_op jit(solution)/shard_map/pallas_call | solution.py:275
  2.5 0.0 copy-start.1
  2.5 14.7 %all_to_all.10 = f32[32,1,640]{2,1,0:T(1,128)S(1)} all-to-all(f32[32,1,640]{2,1,0:T(1,128)S(1)} %bitcast.24), channel_id=1, replica_groups=mesh['clump'=8,'grp'=4] {'clump','grp'}, dimensions={0} | all-to-all | bytes 163840 | tf_op jit(solution)/shard_map/all_to_all | solution.py:244
  17.2 0.0 copy-done.1
  17.2 0.3 %shard_map.143 = (f32[128,128]{1,0:T(8,128)S(1)}, f32[64,128]{1,0:T(8,128)S(1)}) custom-call(f32[160,128]{1,0:T(8,128)S(1)} %bitcast.25, f32[1,128]{1,0:T(1,128)S(1)} %get-tuple-element.23.frac, f32[64,128]{1,0:T(8,128)S(1)} %bitcast.27), custom_call_target="tpu_custom_call" | custom-call | flops 67108864 | bytes 1048576 | tf_op jit(solution)/shard_map/pallas_call | solution.py:281
  17.5 9.1 %all_to_all.11 = f32[32,1,512]{2,1,0:T(1,128)S(1)} all-to-all(f32[32,1,512]{2,1,0:T(1,128)S(1)} %bitcast.26), channel_id=1, replica_groups=mesh['clump'=8,'grp'=4] {'clump','grp'}, dimensions={0} | all-to-all | bytes 131072 | tf_op jit(solution)/shard_map/all_to_all | solution.py:244
  26.6 1.0 %shard_map.144 = (f32[64,128]{1,0:T(8,128)}, f32[64,1024]{1,0:T(8,128)}) custom-call(f32[128,128]{1,0:T(8,128)S(1)} %bitcast.22, s32[8,128]{1,0:T(8,128)S(1)} %get-tuple-element.25.slot, f32[64,1024]{1,0:T(8,128)S(1)} %get-tuple-element.26.kept, f32[64,128]{1,0:T(8,128)S(1)} %get-tuple-element.27.merged), custom_call_target="tpu_custom_call" | custom-call | flops 67108864 | bytes 1048576 | tf_op jit(solution)/shard_map/pallas_call | solution.py:287
  (1 shorter events, 0.0 us)
Async XLA Ops:
  0.6 0.8 %copy-start.2 = (f32[16,64]{1,0:T(8,128)S(1)}, f32[16,64]{1,0:T(8,128)}, u32[]{:S(2)}) copy-start(f32[16,64]{1,0:T(8,128)} %scale.1) | copy-start | bytes 12292
  0.6 0.8 %copy-start.3 = (s32[1,1024]{1,0:T(1,128)S(1)}, s32[1,1024]{1,0:T(1,128)}, u32[]{:S(2)}) copy-start(s32[1,1024]{1,0:T(1,128)} %param.16) | copy-start | bytes 12292
  0.7 0.8 %copy-start.4 = (f32[1,1024]{1,0:T(1,128)S(1)}, f32[1,1024]{1,0:T(1,128)}, u32[]{:S(2)}) copy-start(f32[1,1024]{1,0:T(1,128)} %param.15) | copy-start | bytes 12292
  0.7 0.8 %copy-start.5 = (s32[1,1024]{1,0:T(1,128)S(1)}, s32[1,1024]{1,0:T(1,128)}, u32[]{:S(2)}) copy-start(s32[1,1024]{1,0:T(1,128)} %param.14) | copy-start | bytes 12292
  0.7 0.8 %copy-start.6 = (s32[1,512]{1,0:T(1,128)S(1)}, s32[1,512]{1,0:T(1,128)}, u32[]{:S(2)}) copy-start(s32[1,512]{1,0:T(1,128)} %param.18) | copy-start | bytes 6148
  0.7 0.8 %copy-start.7 = (f32[1,512]{1,0:T(1,128)S(1)}, f32[1,512]{1,0:T(1,128)}, u32[]{:S(2)}) copy-start(f32[1,512]{1,0:T(1,128)} %param.17) | copy-start | bytes 6148
  0.7 0.8 %copy-start.8 = (s32[1,256]{1,0:T(1,128)S(1)}, s32[1,256]{1,0:T(1,128)}, u32[]{:S(2)}) copy-start(s32[1,256]{1,0:T(1,128)} %param.20) | copy-start | bytes 3076
  0.7 0.8 %copy-start.9 = (f32[1,256]{1,0:T(1,128)S(1)}, f32[1,256]{1,0:T(1,128)}, u32[]{:S(2)}) copy-start(f32[1,256]{1,0:T(1,128)} %param.19) | copy-start | bytes 3076
  0.7 0.8 %copy-start.10 = (s32[1,128]{1,0:T(1,128)S(1)}, s32[1,128]{1,0:T(1,128)}, u32[]{:S(2)}) copy-start(s32[1,128]{1,0:T(1,128)} %target.1) | copy-start | bytes 1540
  0.7 0.8 %copy-start.11 = (f32[128]{0:T(128)S(1)}, f32[128]{0:T(128)}, u32[]{:S(2)}) copy-start(f32[128]{0:T(128)} %param.24) | copy-start | bytes 1540
  0.8 1.2 %copy-start = (f32[1,1024,64]{1,2,0:T(8,128)S(1)}, f32[1,1024,64]{1,2,0:T(8,128)}, u32[]{:S(2)}) copy-start(f32[1,1024,64]{1,2,0:T(8,128)} %param.13) | copy-start | bytes 786436
  2.5 14.7 %copy-start.1 = (f32[128,64]{0,1:T(8,128)S(1)}, f32[128,64]{0,1:T(8,128)}, u32[]{:S(2)}) copy-start(f32[128,64]{0,1:T(8,128)} %param.25) | copy-start | bytes 98308

commit v5 on v4

--- a/solution.py
+++ b/solution.py
@@ -8,6 +8,7 @@
 from jax.sharding import PartitionSpec as P
 
 AXES = ("clump", "grp")
+ORDER = ("grp", "clump")
 LANES = 128
 PIECE = 256
 F32, BF16, I32 = jnp.float32, jnp.bfloat16, jnp.int32
@@ -73,7 +74,8 @@
 
 
 def prepare_kernel(
-    n_dev,
+    n_clump,
+    n_group,
     cap,
     pcol,
     clu,
@@ -97,6 +99,7 @@
     frac_out,
 ):
     frac_out[...] = frac[...]
+    n_dev = n_clump * n_group
     cells, patches = home_hot.shape
     nv = live_scale.shape[0]
     groups = LANES // nv
@@ -111,10 +114,11 @@
 
     goal = target[...]
     owner = goal // cells
-    owned = iota((n_dev, cells), 0) == owner
+    seat = owner % n_group * n_clump + owner // n_group
+    owned = iota((n_dev, cells), 0) == seat
     rank = jnp.sum(jnp.where(owned, dot_nn(onehot(owned), before[...]), 0.0), axis=0, keepdims=True)
     rank = rank.astype(I32)
-    slot = (rank % groups * lines + rank // groups) * n_dev + owner
+    slot = (rank % groups * lines + rank // groups) * n_dev + seat
     local = (goal - owner * cells + 1).astype(F32)
     named = jnp.where(owned, local, 0.0).astype(BF16)
     ids[...] = dot_nt(named, onehot(iota((LANES, cells), 0) == rank)) - 1.0
@@ -231,7 +235,8 @@
     cpl_frac,
     cpl_field,
 ):
-    n_dev = lax.axis_size("clump") * lax.axis_size("grp")
+    n_clump, n_group = lax.axis_size("clump"), lax.axis_size("grp")
+    n_dev = n_clump * n_group
     patches, nv = flux.shape[1:]
     cells = cell_target.shape[1]
     cap = max(2, 2 * cells // n_dev)
@@ -240,12 +245,13 @@
 
     def exchange(x):
         rows = x.shape[0] // n_dev
-        x = x.reshape(n_dev, 1, rows * LANES)
-        return lax.all_to_all(x, AXES, split_axis=0, concat_axis=0, tiled=True).reshape(-1, LANES)
+        whole = rows & (rows - 1) == 0
+        x = x.reshape(n_dev, rows, LANES) if whole else x.reshape(n_dev, 1, rows * LANES)
+        return lax.all_to_all(x, ORDER, split_axis=0, concat_axis=0, tiled=True).reshape(-1, LANES)
 
     (before,) = call(order_kernel, [shape((cells, cells), BF16)], [], 1 << 29)()
     *plan, slot, frac = call(
-        functools.partial(prepare_kernel, n_dev, cap),
+        functools.partial(prepare_kernel, n_clump, n_group, cap),
         [
             shape((nv, patches)),
             shape((nv, patches)),

time: 27.9 us -> 27.6 us (0.989)
  blocking collectives: 23.8 us -> 23.5 us
    all_to_all x2, blocking collectives: 23.8 us -> 23.5 us  [exchange(): lax.all_to_all(x, ORDER, split_axis=0, concat_axis=0, tiled=True)]
where the time goes in v5:
time: 27.6 us; the launch traced here: 27.3 us
  blocking collectives  23.5 us (85%)
  Pallas kernels  2.23 us (8%)
  between operations  1.53 us (6%)
    all_to_all x2, blocking collectives, exchange(): lax.all_to_all(x, ORDER, split_axis=0, concat_axis=0, tiled=True)  23.5 us
    pallas_call x1, Pallas kernels, per_device(): call(functools.partial(finish_kernel, n_dev, cap), [shape((nv, cells)), s...  1.01 us

profile of v5, /device:TPU:0, one launch (start us, length us, event | category | flops | bytes accessed | tf_op | source)
XLA Modules:
  0.0 27.3 jit_solution(6999172855290883621)
XLA Ops:
  0.6 0.0 copy-start.2
  0.6 0.0 copy-start.3
  0.7 0.0 copy-start.4
  0.7 0.0 copy-start.5
  0.7 0.0 copy-start.6
  0.7 0.0 copy-start.7
  0.7 0.0 copy-start.8
  0.7 0.0 copy-start.9
  0.7 0.0 copy-start.10
  0.7 0.0 copy-start.11
  0.8 0.0 copy-start
  1.5 0.0 copy-done.2
  1.5 0.0 copy-done.3
  1.5 0.0 copy-done.4
  1.5 0.0 copy-done.5
  1.5 0.0 copy-done.6
  1.5 0.0 copy-done.7
  1.5 0.0 copy-done.8
  1.5 0.0 copy-done.9
  1.5 0.0 copy-done.10
  1.5 0.0 copy-done.11
  1.6 0.4 %shard_map.141 = (f32[64,1024]{1,0:T(8,128)S(1)}, f32[64,1024]{1,0:T(8,128)S(1)}, bf16[128,1024]{1,0:T(8,128)(2,1)S(1)}, bf16[16,1024]{1,0:T(8,128)(2,1)S(1)}, b...) custom-call(s32[8,128]{1,0:T(8,128)S(1)} %bitcast.28, ...), custom_call_target="tpu_custom_call" | custom-call | flops 67108864 | bytes 1048576 | tf_op jit(solution)/shard_map/pallas_call | solution.py:253
  2.0 0.0 copy-done
  2.0 0.5 %shard_map.142 = (f32[160,128]{1,0:T(8,128)S(1)}, f32[64,1024]{1,0:T(8,128)S(1)}) custom-call(f32[64,1024]{1,0:T(8,128)S(1)} %bitcast.23, f32[64,1024]{1,0:T(8,128)S(1)} %get-tuple-element.16.live_scale, f32[64,1024]{1,0:T(8,128)S(1)} %get-tuple-element.17.sum_scale, bf16[128,1024]{1,0:T(8,128)(2,1)S(1)} %get-tuple-element.18.home_hot, ...), custom_call_target="tpu_custom_call" | custom-call | flops 67108864 | bytes 1048576 | tf_op jit(solution)/shard_map/pallas_call | solution.py:281
  2.5 0.0 copy-start.1
  2.5 14.5 %all_to_all.10 = f32[32,1,640]{2,1,0:T(1,128)S(1)} all-to-all(f32[32,1,640]{2,1,0:T(1,128)S(1)} %bitcast.24), channel_id=1, replica_groups=mesh['clump'=8,'grp'=4] {'grp','clump'}, dimensions={0} | all-to-all | bytes 163840 | tf_op jit(solution)/shard_map/all_to_all | solution.py:250
  17.0 0.0 copy-done.1
  17.0 0.3 %shard_map.143 = (f32[128,128]{1,0:T(8,128)S(1)}, f32[64,128]{1,0:T(8,128)S(1)}) custom-call(f32[160,128]{1,0:T(8,128)S(1)} %bitcast.25, f32[1,128]{1,0:T(1,128)S(1)} %get-tuple-element.23.frac, f32[64,128]{1,0:T(8,128)S(1)} %bitcast.27), custom_call_target="tpu_custom_call" | custom-call | flops 67108864 | bytes 1048576 | tf_op jit(solution)/shard_map/pallas_call | solution.py:287
  17.4 9.0 %all_to_all.11 = f32[32,4,128]{2,1,0:T(4,128)S(1)} all-to-all(f32[32,4,128]{2,1,0:T(4,128)S(1)} %bitcast.26), channel_id=1, replica_groups=mesh['clump'=8,'grp'=4] {'grp','clump'}, dimensions={0} | all-to-all | bytes 131072 | tf_op jit(solution)/shard_map/all_to_all | solution.py:250
  26.3 1.0 %shard_map.144 = (f32[64,128]{1,0:T(8,128)}, f32[64,1024]{1,0:T(8,128)}) custom-call(f32[128,128]{1,0:T(8,128)S(1)} %bitcast.22, s32[8,128]{1,0:T(8,128)S(1)} %get-tuple-element.25.slot, f32[64,1024]{1,0:T(8,128)S(1)} %get-tuple-element.26.kept, f32[64,128]{1,0:T(8,128)S(1)} %get-tuple-element.27.merged), custom_call_target="tpu_custom_call" | custom-call | flops 67108864 | bytes 1048576 | tf_op jit(solution)/shard_map/pallas_call | solution.py:293
  (1 shorter events, 0.0 us)
Async XLA Ops:
  0.6 0.8 %copy-start.2 = (f32[16,64]{1,0:T(8,128)S(1)}, f32[16,64]{1,0:T(8,128)}, u32[]{:S(2)}) copy-start(f32[16,64]{1,0:T(8,128)} %scale.1) | copy-start | bytes 12292
  0.6 0.8 %copy-start.3 = (s32[1,1024]{1,0:T(1,128)S(1)}, s32[1,1024]{1,0:T(1,128)}, u32[]{:S(2)}) copy-start(s32[1,1024]{1,0:T(1,128)} %param.16) | copy-start | bytes 12292
  0.7 0.8 %copy-start.4 = (f32[1,1024]{1,0:T(1,128)S(1)}, f32[1,1024]{1,0:T(1,128)}, u32[]{:S(2)}) copy-start(f32[1,1024]{1,0:T(1,128)} %param.15) | copy-start | bytes 12292
  0.7 0.8 %copy-start.5 = (s32[1,1024]{1,0:T(1,128)S(1)}, s32[1,1024]{1,0:T(1,128)}, u32[]{:S(2)}) copy-start(s32[1,1024]{1,0:T(1,128)} %param.14) | copy-start | bytes 12292
  0.7 0.8 %copy-start.6 = (s32[1,512]{1,0:T(1,128)S(1)}, s32[1,512]{1,0:T(1,128)}, u32[]{:S(2)}) copy-start(s32[1,512]{1,0:T(1,128)} %param.18) | copy-start | bytes 6148
  0.7 0.8 %copy-start.7 = (f32[1,512]{1,0:T(1,128)S(1)}, f32[1,512]{1,0:T(1,128)}, u32[]{:S(2)}) copy-start(f32[1,512]{1,0:T(1,128)} %param.17) | copy-start | bytes 6148
  0.7 0.8 %copy-start.8 = (s32[1,256]{1,0:T(1,128)S(1)}, s32[1,256]{1,0:T(1,128)}, u32[]{:S(2)}) copy-start(s32[1,256]{1,0:T(1,128)} %param.20) | copy-start | bytes 3076
  0.7 0.8 %copy-start.9 = (f32[1,256]{1,0:T(1,128)S(1)}, f32[1,256]{1,0:T(1,128)}, u32[]{:S(2)}) copy-start(f32[1,256]{1,0:T(1,128)} %param.19) | copy-start | bytes 3076
  0.7 0.8 %copy-start.10 = (s32[1,128]{1,0:T(1,128)S(1)}, s32[1,128]{1,0:T(1,128)}, u32[]{:S(2)}) copy-start(s32[1,128]{1,0:T(1,128)} %target.1) | copy-start | bytes 1540
  0.7 0.8 %copy-start.11 = (f32[128]{0:T(128)S(1)}, f32[128]{0:T(128)}, u32[]{:S(2)}) copy-start(f32[128]{0:T(128)} %param.24) | copy-start | bytes 1540
  0.8 1.2 %copy-start = (f32[1,1024,64]{1,2,0:T(8,128)S(1)}, f32[1,1024,64]{1,2,0:T(8,128)}, u32[]{:S(2)}) copy-start(f32[1,1024,64]{1,2,0:T(8,128)} %param.13) | copy-start | bytes 786436
  2.5 14.6 %copy-start.1 = (f32[128,64]{0,1:T(8,128)S(1)}, f32[128,64]{0,1:T(8,128)}, u32[]{:S(2)}) copy-start(f32[128,64]{0,1:T(8,128)} %param.25) | copy-start | bytes 98308

commit v6 on v5

--- a/solution.py
+++ b/solution.py
@@ -89,8 +89,8 @@
     scale,
     frac,
     before,
-    live_scale,
-    sum_scale,
+    factor_out,
+    weight_out,
     home_hot,
     weights,
     slot_hot,
@@ -101,7 +101,7 @@
     frac_out[...] = frac[...]
     n_dev = n_clump * n_group
     cells, patches = home_hot.shape
-    nv = live_scale.shape[0]
+    nv = factor_out.shape[0]
     groups = LANES // nv
     lines = cap // groups
 
@@ -129,27 +129,26 @@
     type_hot = onehot(iota((types, patches), 0) == as_row(pft[...]))
     scale_t = jnp.concatenate(split(scale[...]), axis=1).T
     factor = dot_nn(scale_t, type_hot)
-    factor = factor[:nv] + factor[nv:]
     home_row = as_row(jnp.where(alive, home, -1))
     weight_row = as_row(jnp.where(alive, weight, 0.0))
-    live_scale[...] = jnp.where(home_row >= 0, factor, 0.0)
-    sum_scale[...] = factor * weight_row
+    weight_out[...] = weight_row
+    factor_out[...] = jnp.where(home_row >= 0, factor[:nv] + factor[nv:], 0.0)
     home_hot[...] = onehot(iota((cells, patches), 0) == home_row)
     w_high, w_low = split(jnp.broadcast_to(weight_row, weights.shape))
     weights[...] = jnp.where(iota(weights.shape, 0) == 0, w_high, w_low)
 
 
 def local_kernel(
-    n_dev, flux, live_scale, sum_scale, home_hot, weights, slot_hot, ids, send, kept
+    n_dev, flux, factor, weight, home_hot, weights, slot_hot, ids, send, kept
 ):
     nv = flux.shape[0]
     groups = LANES // nv
     part = slot_hot.shape[0] // groups
     lines = part // n_dev
-    values = flux[...]
-    high, low = split(values * sum_scale[...])
+    scaled = flux[...] * factor[...]
+    high, low = split(scaled * weight[...])
     sums = dot_nt(jnp.concatenate([high, low, weights[...]], axis=0), home_hot[...])
-    kept[...] = values * live_scale[...]
+    kept[...] = scaled
     send[pl.ds(lines, n_dev, stride=lines + 1), :] = ids[...]
     den = sums[2 * nv : 2 * nv + 1] + sums[2 * nv + 1 : 2 * nv + 2]
     mean = (sums[:nv] + sums[nv : 2 * nv]) / jnp.maximum(den, 1.0)
@@ -254,7 +253,7 @@
         functools.partial(prepare_kernel, n_clump, n_group, cap),
         [
             shape((nv, patches)),
-            shape((nv, patches)),
+            shape((1, patches)),
             shape((cells, patches), BF16),
             shape((16, patches), BF16),
             shape((n_dev * cap, cells), BF16),

time: 27.6 us -> 27.5 us (level)
  no operation moved by 1% of the time
where the time goes in v6:
time: 27.5 us; the launch traced here: 27.3 us
  blocking collectives  23.5 us (85%)
  Pallas kernels  2.22 us (8%)
  between operations  1.53 us (6%)
    all_to_all x2, blocking collectives, exchange(): lax.all_to_all(x, ORDER, split_axis=0, concat_axis=0, tiled=True)  23.5 us
    pallas_call x1, Pallas kernels, per_device(): call(functools.partial(finish_kernel, n_dev, cap), [shape((nv, cells)), s...  1.01 us

profile of v6, /device:TPU:0, one launch (start us, length us, event | category | flops | bytes accessed | tf_op | source)
XLA Modules:
  0.0 27.3 jit_solution(3396750703657065853)
XLA Ops:
  0.6 0.0 copy-start.2
  0.6 0.0 copy-start.3
  0.7 0.0 copy-start.4
  0.7 0.0 copy-start.5
  0.7 0.0 copy-start.6
  0.7 0.0 copy-start.7
  0.7 0.0 copy-start.8
  0.7 0.0 copy-start.9
  0.7 0.0 copy-start.10
  0.7 0.0 copy-start.11
  0.8 0.0 copy-start
  1.5 0.0 copy-done.2
  1.5 0.0 copy-done.3
  1.5 0.0 copy-done.4
  1.5 0.0 copy-done.5
  1.5 0.0 copy-done.6
  1.5 0.0 copy-done.7
  1.5 0.0 copy-done.8
  1.5 0.0 copy-done.9
  1.5 0.0 copy-done.10
  1.5 0.0 copy-done.11
  1.6 0.4 %shard_map.141 = (f32[64,1024]{1,0:T(8,128)S(1)}, f32[1,1024]{1,0:T(1,128)S(1)}, bf16[128,1024]{1,0:T(8,128)(2,1)S(1)}, bf16[16,1024]{1,0:T(8,128)(2,1)S(1)}, bf...) custom-call(s32[8,128]{1,0:T(8,128)S(1)} %bitcast.28, ...), custom_call_target="tpu_custom_call" | custom-call | flops 67108864 | bytes 1048576 | tf_op jit(solution)/shard_map/pallas_call | solution.py:252
  2.0 0.0 copy-done
  2.0 0.5 %shard_map.142 = (f32[160,128]{1,0:T(8,128)S(1)}, f32[64,1024]{1,0:T(8,128)S(1)}) custom-call(f32[64,1024]{1,0:T(8,128)S(1)} %bitcast.22, f32[64,1024]{1,0:T(8,128)S(1)} %get-tuple-element.16.factor, f32[1,1024]{1,0:T(1,128)S(1)} %get-tuple-element.17.weight, bf16[128,1024]{1,0:T(8,128)(2,1)S(1)} %get-tuple-element.18.home_hot, ...), custom_call_target="tpu_custom_call" | custom-call | flops 67108864 | bytes 1048576 | tf_op jit(solution)/shard_map/pallas_call | solution.py:280
  2.5 0.0 copy-start.1
  2.5 14.5 %all_to_all.10 = f32[32,1,640]{2,1,0:T(1,128)S(1)} all-to-all(f32[32,1,640]{2,1,0:T(1,128)S(1)} %bitcast.24), channel_id=1, replica_groups=mesh['clump'=8,'grp'=4] {'grp','clump'}, dimensions={0} | all-to-all | bytes 163840 | tf_op jit(solution)/shard_map/all_to_all | solution.py:249
  17.0 0.0 copy-done.1
  17.0 0.3 %shard_map.143 = (f32[128,128]{1,0:T(8,128)S(1)}, f32[64,128]{1,0:T(8,128)S(1)}) custom-call(f32[160,128]{1,0:T(8,128)S(1)} %bitcast.25, f32[1,128]{1,0:T(1,128)S(1)} %get-tuple-element.23.frac, f32[64,128]{1,0:T(8,128)S(1)} %bitcast.27), custom_call_target="tpu_custom_call" | custom-call | flops 67108864 | bytes 1048576 | tf_op jit(solution)/shard_map/pallas_call | solution.py:286
  17.3 9.0 %all_to_all.11 = f32[32,4,128]{2,1,0:T(4,128)S(1)} all-to-all(f32[32,4,128]{2,1,0:T(4,128)S(1)} %bitcast.26), channel_id=1, replica_groups=mesh['clump'=8,'grp'=4] {'grp','clump'}, dimensions={0} | all-to-all | bytes 131072 | tf_op jit(solution)/shard_map/all_to_all | solution.py:249
  26.3 1.0 %shard_map.144 = (f32[64,128]{1,0:T(8,128)}, f32[64,1024]{1,0:T(8,128)}) custom-call(f32[128,128]{1,0:T(8,128)S(1)} %bitcast.23, s32[8,128]{1,0:T(8,128)S(1)} %get-tuple-element.25.slot, f32[64,1024]{1,0:T(8,128)S(1)} %get-tuple-element.26.kept, f32[64,128]{1,0:T(8,128)S(1)} %get-tuple-element.27.merged), custom_call_target="tpu_custom_call" | custom-call | flops 67108864 | bytes 1048576 | tf_op jit(solution)/shard_map/pallas_call | solution.py:292
  (1 shorter events, 0.0 us)
Async XLA Ops:
  0.6 0.8 %copy-start.2 = (f32[16,64]{1,0:T(8,128)S(1)}, f32[16,64]{1,0:T(8,128)}, u32[]{:S(2)}) copy-start(f32[16,64]{1,0:T(8,128)} %scale.1) | copy-start | bytes 12292
  0.6 0.8 %copy-start.3 = (s32[1,1024]{1,0:T(1,128)S(1)}, s32[1,1024]{1,0:T(1,128)}, u32[]{:S(2)}) copy-start(s32[1,1024]{1,0:T(1,128)} %param.16) | copy-start | bytes 12292
  0.7 0.8 %copy-start.4 = (f32[1,1024]{1,0:T(1,128)S(1)}, f32[1,1024]{1,0:T(1,128)}, u32[]{:S(2)}) copy-start(f32[1,1024]{1,0:T(1,128)} %param.15) | copy-start | bytes 12292
  0.7 0.8 %copy-start.5 = (s32[1,1024]{1,0:T(1,128)S(1)}, s32[1,1024]{1,0:T(1,128)}, u32[]{:S(2)}) copy-start(s32[1,1024]{1,0:T(1,128)} %param.14) | copy-start | bytes 12292
  0.7 0.8 %copy-start.6 = (s32[1,512]{1,0:T(1,128)S(1)}, s32[1,512]{1,0:T(1,128)}, u32[]{:S(2)}) copy-start(s32[1,512]{1,0:T(1,128)} %param.18) | copy-start | bytes 6148
  0.7 0.8 %copy-start.7 = (f32[1,512]{1,0:T(1,128)S(1)}, f32[1,512]{1,0:T(1,128)}, u32[]{:S(2)}) copy-start(f32[1,512]{1,0:T(1,128)} %param.17) | copy-start | bytes 6148
  0.7 0.8 %copy-start.8 = (s32[1,256]{1,0:T(1,128)S(1)}, s32[1,256]{1,0:T(1,128)}, u32[]{:S(2)}) copy-start(s32[1,256]{1,0:T(1,128)} %param.20) | copy-start | bytes 3076
  0.7 0.8 %copy-start.9 = (f32[1,256]{1,0:T(1,128)S(1)}, f32[1,256]{1,0:T(1,128)}, u32[]{:S(2)}) copy-start(f32[1,256]{1,0:T(1,128)} %param.19) | copy-start | bytes 3076
  0.7 0.8 %copy-start.10 = (s32[1,128]{1,0:T(1,128)S(1)}, s32[1,128]{1,0:T(1,128)}, u32[]{:S(2)}) copy-start(s32[1,128]{1,0:T(1,128)} %target.1) | copy-start | bytes 1540
  0.7 0.8 %copy-start.11 = (f32[128]{0:T(128)S(1)}, f32[128]{0:T(128)}, u32[]{:S(2)}) copy-start(f32[128]{0:T(128)} %param.24) | copy-start | bytes 1540
  0.8 1.2 %copy-start = (f32[1,1024,64]{1,2,0:T(8,128)S(1)}, f32[1,1024,64]{1,2,0:T(8,128)}, u32[]{:S(2)}) copy-start(f32[1,1024,64]{1,2,0:T(8,128)} %param.13) | copy-start | bytes 786436
  2.5 14.6 %copy-start.1 = (f32[128,64]{0,1:T(8,128)S(1)}, f32[128,64]{0,1:T(8,128)}, u32[]{:S(2)}) copy-start(f32[128,64]{0,1:T(8,128)} %param.25) | copy-start | bytes 98308

commit v7 on v5

--- a/solution.py
+++ b/solution.py
@@ -158,7 +158,7 @@
         send[pl.ds(k, n_dev, stride=lines + 1), :] = out[k * n_dev : (k + 1) * n_dev, :]
 
 
-def owner_kernel(n_dev, cap, got, frac, field, send, merged_out):
+def owner_kernel(n_dev, cap, got, frac, field, send, hot_out):
     nv, cells = field.shape
     groups = LANES // nv
     lines = cap // groups
@@ -176,26 +176,30 @@
         at = slice(k * n_dev, (k + 1) * n_dev)
         row = got[pl.ds(k, n_dev, stride=lines + 1), :]
         send[pl.ds(k, n_dev, stride=lines), :] = own[at, :] * row + other[at, :]
-    means = unpack(got, n_dev, lines, lines + 1, nv)
-    placed = dot_nn(means, jnp.concatenate(hots, axis=0))
-    merged_out[...] = part * (placed[:nv] + placed[nv:]) + rest
-
-
-def finish_kernel(n_dev, cap, got, slot, kept, merged, merged_out, anomaly_out, buffer, sem):
+    hot_out[...] = jnp.concatenate(hots, axis=0)
+
+
+def finish_kernel(
+    n_dev, cap, got, slot, kept, heard, hot, frac, field, merged_out, anomaly_out, buffer, merged, sem
+):
     nv, patches = kept.shape
     pieces = buffer.shape[1] // PIECE
-    copies = [pltpu.make_async_copy(merged, merged_out, sem.at[pieces])]
-    copies[0].start()
+    copies = []
     lines = cap * nv // LANES
     replies = unpack(got, n_dev, lines, lines, nv)
     row = as_row(slot[...])
     for c in range(pieces):
         at = slice(c * PIECE, (c + 1) * PIECE)
-        hot = onehot(iota((n_dev * cap, PIECE), 0) == row[:, at])
-        picked = dot_nn(replies, hot)
+        patch_hot = onehot(iota((n_dev * cap, PIECE), 0) == row[:, at])
+        picked = dot_nn(replies, patch_hot)
         buffer[:, at] = kept[:, at] - (picked[:nv] + picked[nv:])
         copies.append(pltpu.make_async_copy(buffer.at[:, at], anomaly_out.at[:, at], sem.at[c]))
         copies[-1].start()
+    placed = dot_nn(unpack(heard, n_dev, lines, lines + 1, nv), hot[...])
+    part = frac[...]
+    merged[...] = part * (placed[:nv] + placed[nv:]) + (1.0 - part) * field[...]
+    copies.append(pltpu.make_async_copy(merged, merged_out, sem.at[pieces]))
+    copies[-1].start()
     for copy in copies:
         copy.wait()
 
@@ -284,20 +288,26 @@
         [VMEM] * 7,
         1 << 26,
     )(flux[0].T, *plan)
-    reply, merged = call(
+    field_t = cpl_field.T
+    heard = exchange(send)
+    reply, hot = call(
         functools.partial(owner_kernel, n_dev, cap),
-        [shape((n_dev * lines, LANES)), shape((nv, cells))],
+        [shape((n_dev * lines, LANES)), shape((n_dev * cap, cells), BF16)],
         [VMEM] * 3,
         1 << 26,
-    )(exchange(send), frac, cpl_field.T)
+    )(heard, frac, field_t)
     merged, anomaly = call(
         functools.partial(finish_kernel, n_dev, cap),
         [shape((nv, cells)), shape((nv, patches))],
-        [VMEM] * 4,
+        [VMEM] * 7,
         1 << 26,
-        [pltpu.VMEM((nv, patches), F32), pltpu.SemaphoreType.DMA((patches // PIECE + 1,))],
+        [
+            pltpu.VMEM((nv, patches), F32),
+            pltpu.VMEM((nv, cells), F32),
+            pltpu.SemaphoreType.DMA((patches // PIECE + 1,)),
+        ],
         HBM,
-    )(exchange(reply), slot, kept, merged)
+    )(exchange(reply), slot, kept, heard, hot, frac, field_t)
     return merged.T, anomaly.T[None]
 
 

time: 27.6 us -> 27.5 us (level)
  no operation moved by 1% of the time
where the time goes in v7:
time: 27.5 us; the launch traced here: 27.3 us
  blocking collectives  23.5 us (85%)
  Pallas kernels  2.2 us (8%)
  between operations  1.53 us (6%)
    all_to_all x2, blocking collectives, exchange(): lax.all_to_all(x, ORDER, split_axis=0, concat_axis=0, tiled=True)  23.5 us
    pallas_call x1, Pallas kernels, per_device(): call(functools.partial(finish_kernel, n_dev, cap), [shape((nv, cells)), s...  1.02 us

profile of v7, /device:TPU:0, one launch (start us, length us, event | category | flops | bytes accessed | tf_op | source)
XLA Modules:
  0.0 27.3 jit_solution(16100699549326588752)
XLA Ops:
  0.6 0.0 copy-start.2
  0.6 0.0 copy-start.3
  0.7 0.0 copy-start.4
  0.7 0.0 copy-start.5
  0.7 0.0 copy-start.6
  0.7 0.0 copy-start.7
  0.7 0.0 copy-start.8
  0.7 0.0 copy-start.9
  0.7 0.0 copy-start.10
  0.7 0.0 copy-start.11
  0.8 0.0 copy-start
  1.5 0.0 copy-done.2
  1.5 0.0 copy-done.3
  1.5 0.0 copy-done.4
  1.5 0.0 copy-done.5
  1.5 0.0 copy-done.6
  1.5 0.0 copy-done.7
  1.5 0.0 copy-done.8
  1.5 0.0 copy-done.9
  1.5 0.0 copy-done.10
  1.5 0.0 copy-done.11
  1.6 0.4 %shard_map.141 = (f32[64,1024]{1,0:T(8,128)S(1)}, f32[64,1024]{1,0:T(8,128)S(1)}, bf16[128,1024]{1,0:T(8,128)(2,1)S(1)}, bf16[16,1024]{1,0:T(8,128)(2,1)S(1)}, b...) custom-call(s32[8,128]{1,0:T(8,128)S(1)} %bitcast.30, ...), custom_call_target="tpu_custom_call" | custom-call | flops 67108864 | bytes 1048576 | tf_op jit(solution)/shard_map/pallas_call | solution.py:257
  2.0 0.0 copy-done
  2.0 0.5 %shard_map.142 = (f32[160,128]{1,0:T(8,128)S(1)}, f32[64,1024]{1,0:T(8,128)S(1)}) custom-call(f32[64,1024]{1,0:T(8,128)S(1)} %bitcast.25, f32[64,1024]{1,0:T(8,128)S(1)} %get-tuple-element.16.live_scale, f32[64,1024]{1,0:T(8,128)S(1)} %get-tuple-element.17.sum_scale, bf16[128,1024]{1,0:T(8,128)(2,1)S(1)} %get-tuple-element.18.home_hot, ...), custom_call_target="tpu_custom_call" | custom-call | flops 67108864 | bytes 1048576 | tf_op jit(solution)/shard_map/pallas_call | solution.py:285
  2.5 0.0 copy-start.1
  2.5 14.5 %all_to_all.10 = f32[32,1,640]{2,1,0:T(1,128)S(1)} all-to-all(f32[32,1,640]{2,1,0:T(1,128)S(1)} %bitcast.26), channel_id=1, replica_groups=mesh['clump'=8,'grp'=4] {'grp','clump'}, dimensions={0} | all-to-all | bytes 163840 | tf_op jit(solution)/shard_map/all_to_all | solution.py:254
  17.0 0.0 copy-done.1
  17.0 0.3 shard_map.143
  17.3 9.0 %all_to_all.11 = f32[32,4,128]{2,1,0:T(4,128)S(1)} all-to-all(f32[32,4,128]{2,1,0:T(4,128)S(1)} %bitcast.27), channel_id=1, replica_groups=mesh['clump'=8,'grp'=4] {'grp','clump'}, dimensions={0} | all-to-all | bytes 131072 | tf_op jit(solution)/shard_map/all_to_all | solution.py:254
  26.3 1.0 %shard_map.144 = (f32[64,128]{1,0:T(8,128)}, f32[64,1024]{1,0:T(8,128)}) custom-call(f32[128,128]{1,0:T(8,128)S(1)} %bitcast.24, s32[8,128]{1,0:T(8,128)S(1)} %get-tuple-element.25.slot, f32[64,1024]{1,0:T(8,128)S(1)} %get-tuple-element.26.kept, f32[160,128]{1,0:T(8,128)S(1)} %bitcast.23, bf16[256,128]{1,0:T(8,128)(2,1)S(1)} %get-tuple-element.27.hot, ...), custom_call_target="tpu_custom_call" | custom-call | flops 67108864 | bytes 1048576 | tf_op jit(solution)/shard_map/pallas_call | solution.py:299
  (1 shorter events, 0.0 us)
Async XLA Ops:
  0.6 0.8 %copy-start.2 = (f32[16,64]{1,0:T(8,128)S(1)}, f32[16,64]{1,0:T(8,128)}, u32[]{:S(2)}) copy-start(f32[16,64]{1,0:T(8,128)} %scale.1) | copy-start | bytes 12292
  0.6 0.8 %copy-start.3 = (s32[1,1024]{1,0:T(1,128)S(1)}, s32[1,1024]{1,0:T(1,128)}, u32[]{:S(2)}) copy-start(s32[1,1024]{1,0:T(1,128)} %param.16) | copy-start | bytes 12292
  0.7 0.8 %copy-start.4 = (f32[1,1024]{1,0:T(1,128)S(1)}, f32[1,1024]{1,0:T(1,128)}, u32[]{:S(2)}) copy-start(f32[1,1024]{1,0:T(1,128)} %param.15) | copy-start | bytes 12292
  0.7 0.8 %copy-start.5 = (s32[1,1024]{1,0:T(1,128)S(1)}, s32[1,1024]{1,0:T(1,128)}, u32[]{:S(2)}) copy-start(s32[1,1024]{1,0:T(1,128)} %param.14) | copy-start | bytes 12292
  0.7 0.8 %copy-start.6 = (s32[1,512]{1,0:T(1,128)S(1)}, s32[1,512]{1,0:T(1,128)}, u32[]{:S(2)}) copy-start(s32[1,512]{1,0:T(1,128)} %param.18) | copy-start | bytes 6148
  0.7 0.8 %copy-start.7 = (f32[1,512]{1,0:T(1,128)S(1)}, f32[1,512]{1,0:T(1,128)}, u32[]{:S(2)}) copy-start(f32[1,512]{1,0:T(1,128)} %param.17) | copy-start | bytes 6148
  0.7 0.8 %copy-start.8 = (s32[1,256]{1,0:T(1,128)S(1)}, s32[1,256]{1,0:T(1,128)}, u32[]{:S(2)}) copy-start(s32[1,256]{1,0:T(1,128)} %param.20) | copy-start | bytes 3076
  0.7 0.8 %copy-start.9 = (f32[1,256]{1,0:T(1,128)S(1)}, f32[1,256]{1,0:T(1,128)}, u32[]{:S(2)}) copy-start(f32[1,256]{1,0:T(1,128)} %param.19) | copy-start | bytes 3076
  0.7 0.8 %copy-start.10 = (s32[1,128]{1,0:T(1,128)S(1)}, s32[1,128]{1,0:T(1,128)}, u32[]{:S(2)}) copy-start(s32[1,128]{1,0:T(1,128)} %target.1) | copy-start | bytes 1540
  0.7 0.8 %copy-start.11 = (f32[128]{0:T(128)S(1)}, f32[128]{0:T(128)}, u32[]{:S(2)}) copy-start(f32[128]{0:T(128)} %param.24) | copy-start | bytes 1540
  0.8 1.2 %copy-start = (f32[1,1024,64]{1,2,0:T(8,128)S(1)}, f32[1,1024,64]{1,2,0:T(8,128)}, u32[]{:S(2)}) copy-start(f32[1,1024,64]{1,2,0:T(8,128)} %param.13) | copy-start | bytes 786436
  2.5 14.6 %copy-start.1 = (f32[128,64]{0,1:T(8,128)S(1)}, f32[128,64]{0,1:T(8,128)}, u32[]{:S(2)}) copy-start(f32[128,64]{0,1:T(8,128)} %param.25) | copy-start | bytes 98308
